TPU v7x, 128 devices: a whole 4x4x4 slice. The times are simulated.
128 devices in a mesh: part: 1, row: 2 (over core), col: 64 (over z, y, x).
Axes of the slice: x: 4, y: 4, z: 4, core: 2. Of those that a mesh axis runs over, the one named last changes fastest.
Arguments:
- ratings: float32 [4096, 32768], P(('part', 'row'), 'col')
- mask: int32 [4096, 32768], P(('part', 'row'), 'col')
- v_init: float32 [32768, 50], P(('part', 'col'))
Outputs:
- output 1: float32 [4096, 50], P(('part', 'row', 'col'))
- output 2: float32 [32768, 50], P(('part', 'col', 'row'))
All inputs are finite; a program needn't handle non-finite values.
Results may differ from a plain program's by a relative error of at most 0.001.
Values are sent between devices in bfloat16 or wider.
A program may use at most 1 GiB of HBM per device.

v0:
```python
import jax
import jax.numpy as jnp
from jax import lax
from jax.sharding import PartitionSpec as P

RIDGE_WEIGHT = 0.05


def solve_rows(gram, rhs):
    row_count, width = rhs.shape
    gram_mats = gram.reshape(row_count, width, width) + RIDGE_WEIGHT * jnp.eye(width, dtype=jnp.float32)
    chol_fac = jnp.linalg.cholesky(gram_mats)
    fwd_sol = lax.linalg.triangular_solve(chol_fac, rhs[:, :, None], left_side=True, lower=True)
    solved = lax.linalg.triangular_solve(chol_fac, fwd_sol, left_side=True, lower=True, transpose_a=True)
    return solved[:, :, 0]


def outer_rows(fac_b):
    row_count, width = fac_b.shape
    return (fac_b[:, :, None] * fac_b[:, None, :]).reshape(row_count, width * width)


def solution(mesh):
    block_spec = P(("part", "row"), "col")
    in_specs = (block_spec, block_spec, P(("part", "col"), None))
    out_specs = (P(("part", "row", "col"), None), P(("part", "col", "row"), None))
    contract_rows = (((0,), (0,)), ((), ()))

    def local_als(ratings, mask, v_init):
        mask_b = mask.astype(jnp.bfloat16)
        rated_b = jnp.where(mask != 0, ratings, 0.0).astype(jnp.bfloat16)
        v_b = v_init.astype(jnp.bfloat16)
        gram_part = jnp.dot(mask_b, outer_rows(v_b), preferred_element_type=jnp.float32)
        rhs_part = jnp.dot(rated_b, v_b, preferred_element_type=jnp.float32)
        gram_own = lax.psum_scatter(gram_part, "col", scatter_dimension=0, tiled=True)
        rhs_own = lax.psum_scatter(rhs_part, "col", scatter_dimension=0, tiled=True)
        w_own = solve_rows(gram_own, rhs_own)
        w_rows = lax.all_gather(w_own.astype(jnp.bfloat16), "col", axis=0, tiled=True)
        gram_item = lax.dot_general(mask_b, outer_rows(w_rows), contract_rows, preferred_element_type=jnp.float32)
        rhs_item = lax.dot_general(rated_b, w_rows, contract_rows, preferred_element_type=jnp.float32)
        gram_iown = lax.psum_scatter(gram_item, "row", scatter_dimension=0, tiled=True)
        rhs_iown = lax.psum_scatter(rhs_item, "row", scatter_dimension=0, tiled=True)
        v_own = solve_rows(gram_iown, rhs_iown)
        return w_own, v_own

    return jax.shard_map(local_als, mesh=mesh, in_specs=in_specs, out_specs=out_specs, check_vma=False)
```

profile of v0, /device:TPU:1, one launch (start us, length us, event | category | flops | bytes accessed | tf_op | source)
XLA Modules:
  0.0 2324.6 jit_solution(11249692763757978202)
XLA Ops:
  8.3 2.1 mul.43
  10.4 12.1 convolution_bitcast_fusion
  22.5 19.8 copy.72
  42.4 4.6 select_convert_fusion
  46.9 1.7 fusion.6
  48.9 358.4 %reduce-scatter.13.cloned.1.call-done = f32[32,2500]{1,0:T(8,128)} async-done(((f32[2048,2500]{1,0:T(8,128)}), f32[32,2500]{1,0:T(8,128)}) %reduce-scatter.13.cloned.1.call-update) | async-done | bytes 320016
  407.3 2.3 reshape.81
  409.5 1.3 copy_add_fusion
  410.9 1.6 copy.43
  412.4 2.7 fusion.5
  415.1 148.1 %custom-call.18 = f32[32,50,50]{2,1,0:T(8,128)} custom-call(f32[32,50,50]{2,1,0:T(8,128)} %fusion.5), custom_call_target="Cholesky" | custom-call | tf_op jit(solution)/shard_map/jit(cholesky)/cholesky | solution.py:12
  563.3 1.7 copy.45
  565.7 1.5 select_bitcast_fusion.1
  567.2 40.1 %custom-call.19 = f32[32,1,50,50]{0,2,3,1:T(8,128)} custom-call(f32[32,1,50,50]{0,3,2,1:T(8,128)} %select_bitcast_fusion.1), custom_call_target="InvertDiagBlocksLowerTriangular" | custom-call | tf_op jit(solution)/shard_map/triangular_solve | solution.py:14
  607.2 1.9 copy.56
  609.2 146.4 %reduce-scatter.7.cloned.1.call-done = f32[32,50]{1,0:T(8,128)} async-done(((f32[2048,50]{1,0:T(8,128)}), f32[32,50]{1,0:T(8,128)}) %reduce-scatter.7.cloned.1.call-update) | async-done | bytes 6416 | tf_op jit(solution)/shard_map/reduce_scatter | solution.py:36
  755.6 1.6 convolution_bitcast_fusion.2
  757.3 1.5 fusion.7
  758.8 146.7 %all_gather.3 = bf16[2048,50]{1,0:T(8,128)(2,1)S(1)} all-gather(bf16[32,50]{1,0:T(8,128)(2,1)S(1)} %convert_element_type.17), channel_id=1, replica_groups=mesh['part'=1,'row'=2,'col'=64] {'col'}, dimensions={0}, use_global_device_ids=true | all-gather | bytes 208000 | tf_op jit(solution)/shard_map/all_gather | solution.py:38
  905.8 5.3 broadcast_multiply_fusion
  911.0 13.9 mul.48
  924.9 10.9 convolution_bitcast_fusion.1
  937.3 85.7 %reduce-scatter.9.cloned.1.call-done = f32[256,2500]{0,1:T(8,128)} async-done(((f32[512,2500]{0,1:T(8,128)}), f32[256,2500]{0,1:T(8,128)}) %reduce-scatter.9.cloned.1.call-update) | async-done | bytes 2560016 | tf_op jit(solution)/shard_map/reduce_scatter | solution.py:41
  1023.0 3.7 reshape.69
  1026.7 2.2 broadcast_add_fusion
  1028.9 7.7 copy.49
  1036.6 8.7 copy.50
  1045.3 8.9 fusion
  1054.3 1175.7 %custom-call.20 = f32[256,50,50]{2,1,0:T(8,128)} custom-call(f32[256,50,50]{2,1,0:T(8,128)} %fusion), custom_call_target="Cholesky" | custom-call | tf_op jit(solution)/shard_map/jit(cholesky)/cholesky | solution.py:12
  2230.0 6.6 copy.51
  2237.2 1.9 select_bitcast_fusion
  2239.1 76.9 %custom-call.21 = f32[256,1,50,50]{0,2,3,1:T(8,128)S(1)} custom-call(f32[256,1,50,50]{0,3,2,1:T(8,128)} %select_bitcast_fusion), custom_call_target="InvertDiagBlocksLowerTriangular" | custom-call | tf_op jit(solution)/shard_map/triangular_solve | solution.py:14
  (29 shorter events, 6.5 us)
Async XLA Ops:
  7.2 400.1 %reduce-scatter.13.cloned.1.call-start = ((), (), s32[]{:S(2)}) async-start(), calls=%async_computation.7 | async-start | bytes 21299200
  42.3 713.3 %reduce-scatter.7.cloned.1.call-start = ((), (), s32[]{:S(2)}) async-start(), calls=%async_computation.4 | async-start | bytes 1064960 | tf_op jit(solution)/shard_map/reduce_scatter | solution.py:36
  48.6 974.4 %reduce-scatter.9.cloned.1.call-start = ((), (), s32[]{:S(2)}) async-start(), calls=%async_computation.5 | async-start | bytes 7692288 | tf_op jit(solution)/shard_map/reduce_scatter | solution.py:41
  48.9 366.3 %copy-start = (f32[50,50]{1,0:T(8,128)}, f32[50,50]{1,0:T(8,128)S(1)}, u32[]{:S(2)}) copy-start(f32[50,50]{1,0:T(8,128)S(1)} %broadcast_select_fusion) | copy-start | bytes 30004
  758.8 152.3 %copy-start.2 = (f32[32,1,50]{2,1,0:T(1,128)}, f32[32,1,50]{2,1,0:T(1,128)S(1)}, u32[]{:S(2)}) copy-start(f32[32,1,50]{2,1,0:T(1,128)S(1)} %fusion.7) | copy-start | bytes 19204
  935.9 1380.1 %reduce-scatter.11.cloned.1.call-start = ((), (), s32[]{:S(2)}) async-start(), calls=%async_computation.6 | async-start | bytes 172032 | tf_op jit(solution)/shard_map/reduce_scatter | solution.py:42
  937.3 89.4 %copy-start.1 = (f32[50,50]{1,0:T(8,128)S(1)}, f32[50,50]{1,0:T(8,128)}, u32[]{:S(2)}) copy-start(f32[50,50]{1,0:T(8,128)} %copy-done) | copy-start | bytes 30004
Sparse Core Ops, SparseCore 0:
  42.4 364.7 reduce-scatter.12
  409.6 345.9 reduce-scatter.6
  936.0 86.9 reduce-scatter.8
  1025.2 11.5 reduce-scatter.10
where the time goes:
time: 2330 us; the launch traced here: 2320 us
  other arithmetic  1470 us (63%)
  waiting for transfers between devices  591 us (25%)
  blocking collectives  147 us (6%)
  local copies, waits for them, and re-layouts  70.2 us (3%)
  matrix products  29 us (1%)
    another operation x7, other arithmetic, solve_rows(): chol_fac = jnp.linalg.cholesky(gram_mats)  1330 us
    unnamed x5, waiting for transfers between devices  358 us
    all_gather x1, blocking collectives, local_als(): lax.all_gather(w_own.astype(jnp.bfloat16), 'col', axis=0, tiled=True)  147 us
    reduce_scatter x1, waiting for transfers between devices, local_als(): rhs_own = lax.psum_scatter(rhs_part, 'col', scatter_dimension=0, tiled=True)  146 us
    another operation x6, other arithmetic, solve_rows(): lax.linalg.triangular_solve(chol_fac, fwd_sol, left_side=True, lower=True...  121 us
    reduce_scatter x1, waiting for transfers between devices, local_als(): lax.psum_scatter(gram_item, 'row', scatter_dimension=0, tiled=True)  85.7 us
  transfers between devices with their start and end apart: 4, of which 3 were waited for; matrix products, arithmetic and copies ran while one was open for 65% of the time, Pallas kernels for 0%

commit v1 on v0

v1 whole, which is shorter than its diff:
```python
import jax
import jax.numpy as jnp
from jax import lax
from jax.experimental import pallas as pl
from jax.experimental.pallas import tpu as pltpu
from jax.sharding import PartitionSpec as P

RIDGE_WEIGHT = 0.05
WIDTH = 50
ROWS = 56
TRI = 1280
LANES = 128


def tri_off(j):
    return j * WIDTH - j * (j - 1) // 2


def outer_tile(vt, dst):
    lanes = vt.shape[1]
    for j in range(WIDTH):
        rows = WIDTH - j
        dst[tri_off(j):tri_off(j) + rows, :] = vt[j:WIDTH, :] * vt[j:j + 1, :]


def outer_kernel(vt_ref, out_ref, tmp):
    tmp[1272:1280, :] = jnp.zeros((8, tmp.shape[1]), jnp.float32)
    outer_tile(vt_ref, tmp)
    out_ref[...] = tmp[...].astype(jnp.bfloat16)


def outer_rows(vt):
    n = vt.shape[1]
    step = min(n, 512)
    return pl.pallas_call(
        outer_kernel,
        out_shape=jax.ShapeDtypeStruct((TRI, n), jnp.bfloat16),
        grid=(n // step,),
        in_specs=[pl.BlockSpec((64, step), lambda i: (0, i))],
        out_specs=pl.BlockSpec((TRI, step), lambda i: (0, i)),
        scratch_shapes=[pltpu.VMEM((TRI, step), jnp.float32)],
    )(vt)


def solve_tile(g_ref, rhs, fac, inv, sol):
    lanes = fac.shape[1]
    for pan in range(7):
        first = 8 * pan
        rows = ROWS - first
        count = min(8, WIDTH - first)
        ids = lax.broadcasted_iota(jnp.int32, (rows, lanes), 0)
        accs = []
        for c in range(count):
            j = first + c
            start = tri_off(j) - c
            if j < WIDTH - 1:
                raw = g_ref[start:start + rows, :]
            else:
                raw = jnp.broadcast_to(g_ref[tri_off(j):tri_off(j) + 1, :], (rows, lanes))
            col = jnp.where(ids < WIDTH - first, raw, 0.0)
            col = jnp.where(ids == c, col + RIDGE_WEIGHT, col)
            col = jnp.where(ids == WIDTH - first, rhs(j), col)
            accs.append(col)
        if pan:
            def body(k, accs):
                base = pl.multiple_of(k * ROWS, 8)
                left = fac[pl.ds(base + first, rows), :]
                return tuple(
                    acc - left * fac[pl.ds(base + first + c, 1), :] for c, acc in enumerate(accs)
                )
            accs = list(lax.fori_loop(0, first, body, tuple(accs), unroll=2))
        for c in range(count):
            j = first + c
            diag = accs[c][c:c + 1, :]
            root = lax.rsqrt(diag)
            root = root * (1.5 - 0.5 * (diag * root) * root)
            inv[j:j + 1, :] = root
            col = accs[c] * root
            fac[pl.ds(j * ROWS + first, rows), :] = col
            for later in range(c + 1, count):
                accs[later] = accs[later] - col * col[later:later + 1, :]
    sol[48:56, :] = jnp.zeros((8, lanes), jnp.float32)
    for pan in reversed(range(7)):
        first = 8 * pan
        count = min(8, WIDTH - first)
        left = []
        for c in range(count):
            j = first + c
            val = fac[j * ROWS + WIDTH:j * ROWS + WIDTH + 1, :]
            if pan < 6:
                dot = fac[j * ROWS + first + 8:j * ROWS + ROWS, :] * sol[first + 8:ROWS, :]
                val = val - jnp.sum(dot, axis=0, keepdims=True)
            left.append(val)
        for c in reversed(range(count)):
            j = first + c
            got = left[c] * inv[j:j + 1, :]
            sol[j:j + 1, :] = got
            for early in range(c):
                row = (first + early) * ROWS + j
                left[early] = left[early] - fac[row:row + 1, :] * got


def solve_kernel(g_ref, b_ref, out_ref, fac, inv, sol):
    solve_tile(g_ref, lambda j: b_ref[j:j + 1, :], fac, inv, sol)
    out_ref[...] = sol[...]


def solve_rows(gram, rhs):
    n = gram.shape[1]
    return pl.pallas_call(
        solve_kernel,
        out_shape=jax.ShapeDtypeStruct((ROWS, n), jnp.float32),
        grid=(n // LANES,),
        in_specs=[pl.BlockSpec((TRI, LANES), lambda i: (0, i)), pl.BlockSpec((ROWS, LANES), lambda i: (0, i))],
        out_specs=pl.BlockSpec((ROWS, LANES), lambda i: (0, i)),
        scratch_shapes=[
            pltpu.VMEM((WIDTH * ROWS, LANES), jnp.float32),
            pltpu.VMEM((ROWS, LANES), jnp.float32),
            pltpu.VMEM((ROWS, LANES), jnp.float32),
        ],
    )(gram, rhs)


def solution(mesh):
    block_spec = P(("part", "row"), "col")
    in_specs = (block_spec, block_spec, P(("part", "col"), None))
    out_specs = (P(("part", "row", "col"), None), P(("part", "col", "row"), None))
    contract_cols = (((1,), (1,)), ((), ()))
    contract_rows = (((1,), (0,)), ((), ()))

    def local_als(ratings, mask, v_init):
        mask_b = mask.astype(jnp.bfloat16)
        rated_b = jnp.where(mask != 0, ratings, 0.0).astype(jnp.bfloat16)
        v_b = v_init.T.astype(jnp.bfloat16)
        vt = jnp.pad(v_b.astype(jnp.float32), ((0, 64 - WIDTH), (0, 0)))
        contract_items = (((1,), (1,)), ((), ()))
        gram_part = lax.dot_general(mask_b, outer_rows(vt), contract_items, preferred_element_type=jnp.float32)
        rhs_part = lax.dot_general(rated_b, v_b, contract_items, preferred_element_type=jnp.float32)
        both = jnp.concatenate([gram_part, rhs_part], axis=1)
        own = lax.psum_scatter(both, "col", scatter_dimension=0, tiled=True).T
        own = jnp.pad(own, ((0, ROWS - WIDTH), (0, LANES - own.shape[1])))
        w_own = solve_rows(own[:TRI], own[TRI:])[:WIDTH, :32].T
        w_rows = lax.all_gather(w_own.astype(jnp.bfloat16), "col", axis=0, tiled=True)
        wt = jnp.pad(w_rows.T, ((0, 64 - WIDTH), (0, 0)))
        gram_item = lax.dot_general(outer_rows(wt.astype(jnp.float32)), mask_b, contract_rows, preferred_element_type=jnp.float32)
        rhs_item = lax.dot_general(wt[:ROWS], rated_b, contract_rows, preferred_element_type=jnp.float32)
        both_item = jnp.concatenate([gram_item, rhs_item], axis=0)
        iown = lax.psum_scatter(both_item, "row", scatter_dimension=1, tiled=True)
        v_own = solve_rows(iown[:TRI], iown[TRI:])[:WIDTH].T
        return w_own, v_own

    return jax.shard_map(local_als, mesh=mesh, in_specs=in_specs, out_specs=out_specs, check_vma=False)
```

time: 2330 us -> 643 us (0.28)
  other arithmetic: 1470 us -> 15 us
  waiting for transfers between devices: 591 us -> 413 us
  local copies, waits for them, and re-layouts: 70.2 us -> 22.9 us
    another operation x13 -> x0, other arithmetic: 1450 us -> none  [the longest x7 1330 us: solve_rows(): chol_fac = jnp.linalg.cholesky(gram_mats)]
    reduce_scatter x3 -> x1, waiting for transfers between devices: 232 us -> 80.4 us  [local_als(): iown = lax.psum_scatter(both_item, 'row', scatter_dimension=1, tiled=True)]
    unnamed x5 -> x3, waiting for transfers between devices: 358 us -> 332 us
  transfers between devices with their start and end apart: 4 -> 2, of which waited for: 3 -> 2; matrix products, arithmetic and copies ran while one was open for 65% -> 0% of each run, Pallas kernels for 0% -> 0%
where the time goes in v1:
time: 643 us; the launch traced here: 642 us
  waiting for transfers between devices  413 us (64%)
  blocking collectives  148 us (23%)
  local copies, waits for them, and re-layouts  22.9 us (4%)
  Pallas kernels  19 us (3%)
  other arithmetic  15 us (2%)
  between operations  14.1 us (2%)
  matrix products  10.2 us (2%)
    unnamed x3, waiting for transfers between devices  332 us
    all_gather x1, blocking collectives, local_als(): lax.all_gather(w_own.astype(jnp.bfloat16), 'col', axis=0, tiled=True)  148 us
    reduce_scatter x1, waiting for transfers between devices, local_als(): iown = lax.psum_scatter(both_item, 'row', scatter_dimension=1, tiled=True)  80.4 us
    unnamed x11, local copies, waits for them, and re-layouts  15 us
  transfers between devices with their start and end apart: 2, of which 2 were waited for; matrix products, arithmetic and copies ran while one was open for 0% of the time, Pallas kernels for 0%

profile of v1, /device:TPU:1, one launch (start us, length us, event | category | flops | bytes accessed | tf_op | source)
XLA Modules:
  0.0 641.9 jit_solution(352812516343625817)
XLA Ops:
  7.2 0.0 reduce-scatter.7.cloned.1.call-start
  7.2 0.9 convert_bitcast_fusion
  8.1 0.7 pad_convert_fusion.1.vt_ref
  8.8 2.4 shard_map.50
  11.2 4.7 select_convert_fusion
  16.0 0.7 fusion.4
  16.7 0.6 copy-done.1
  17.3 3.0 convolution_bitcast_fusion
  20.3 6.0 pad_maximum_fusion
  26.3 11.8 %copy.12 = f32[2048,1330]{1,0:T(8,128)} copy(f32[2048,1330]{0,1:T(8,128)} %pad_maximum_fusion) | data formatting | bytes 21790720
  38.2 0.0 reduce-scatter.5.cloned.1.call-start
  38.2 332.4 %reduce-scatter.7.cloned.1.call-done = f32[32,1330]{1,0:T(8,128)} async-done(((f32[2048,1330]{1,0:T(8,128)}), f32[32,1330]{1,0:T(8,128)}) %reduce-scatter.7.cloned.1.call-update) | async-done | bytes 170256
  370.6 1.2 copy.13
  371.8 0.6 pad_slice_fusion.b_ref
  372.4 0.9 pad_slice_fusion.1.g_ref
  373.3 4.4 shard_map.51
  377.7 0.8 fusion.7
  378.4 0.1 copy.9
  378.5 147.8 %all_gather.3 = bf16[2048,50]{1,0:T(8,128)(2,1)S(1)} all-gather(bf16[32,50]{1,0:T(8,128)(2,1)S(1)} %copy.9), channel_id=1, replica_groups=mesh['part'=1,'row'=2,'col'=64] {'col'}, dimensions={0}, use_global_device_ids=true | all-gather | bytes 208000 | tf_op jit(solution)/shard_map/all_gather | solution.py:143
  526.3 0.2 copy.10
  526.6 0.4 fusion.3
  527.0 0.9 pad_convert_fusion.vt_ref
  527.9 5.0 shard_map.52
  532.9 6.0 fusion
  538.9 1.8 pad_maximum_fusion.1
  540.8 0.7 copy-done.3
  541.5 0.7 copy.11
  542.2 80.4 %reduce-scatter.5.cloned.1.call-done = f32[1336,256]{1,0:T(8,128)} async-done(((f32[1336,512]{1,0:T(8,128)}), f32[1336,256]{1,0:T(8,128)}) %reduce-scatter.5.cloned.1.call-update) | async-done | bytes 1368080 | tf_op jit(solution)/shard_map/reduce_scatter | solution.py:148
  622.5 1.4 slice.30.b_ref
  624.0 2.5 slice.29.g_ref
  626.4 7.1 %shard_map.53 = f32[56,256]{1,0:T(8,128)} custom-call(f32[1280,256]{1,0:T(8,128)} %slice.29.g_ref, f32[56,256]{1,0:T(8,128)} %slice.30.b_ref), custom_call_target="tpu_custom_call" | custom-call | tf_op jit(solution)/shard_map/pallas_call | solution.py:110
  633.6 1.4 slice_bitcast_fusion
  (9 shorter events, 0.0 us)
Async XLA Ops:
  7.2 363.4 %reduce-scatter.7.cloned.1.call-start = ((), (), s32[]{:S(2)}) async-start(), calls=%async_computation.3 | async-start | bytes 11714560
  11.2 4.7 copy-start.2
  11.2 5.5 copy-start
  16.0 1.3 copy-start.1
  38.2 584.4 %reduce-scatter.5.cloned.1.call-start = ((), (), s32[]{:S(2)}) async-start(), calls=%async_computation.2 | async-start | bytes 4104192 | tf_op jit(solution)/shard_map/reduce_scatter | solution.py:148
  540.7 0.7 copy-start.3
Sparse Core Ops, SparseCore 0:
  38.3 332.2 reduce-scatter.6
  540.9 81.6 reduce-scatter.4

commit v2 on v1

v2 whole, which is shorter than its diff:
```python
import jax
import jax.numpy as jnp
from jax import lax
from jax.experimental import pallas as pl
from jax.experimental.pallas import tpu as pltpu
from jax.sharding import PartitionSpec as P

RIDGE_WEIGHT = 0.05
WIDTH = 50
ROWS = 56
TRI = 1280
LANES = 128


def tri_off(j):
    return j * WIDTH - j * (j - 1) // 2


def outer_tile(vt, dst):
    lanes = vt.shape[1]
    for j in range(WIDTH):
        rows = WIDTH - j
        dst[tri_off(j):tri_off(j) + rows, :] = vt[j:WIDTH, :] * vt[j:j + 1, :]


def solve_tile(g_ref, rhs, fac, inv, sol):
    lanes = fac.shape[1]
    for pan in range(7):
        first = 8 * pan
        rows = ROWS - first
        count = min(8, WIDTH - first)
        ids = lax.broadcasted_iota(jnp.int32, (rows, lanes), 0)
        accs = []
        for c in range(count):
            j = first + c
            start = tri_off(j) - c
            if j < WIDTH - 1:
                raw = g_ref[start:start + rows, :]
            else:
                raw = jnp.broadcast_to(g_ref[tri_off(j):tri_off(j) + 1, :], (rows, lanes))
            col = jnp.where(ids < WIDTH - first, raw, 0.0)
            col = jnp.where(ids == c, col + RIDGE_WEIGHT, col)
            col = jnp.where(ids == WIDTH - first, rhs(j), col)
            accs.append(col)
        if pan:
            def body(k, accs):
                base = pl.multiple_of(k * ROWS, 8)
                left = fac[pl.ds(base + first, rows), :]
                return tuple(
                    acc - left * fac[pl.ds(base + first + c, 1), :] for c, acc in enumerate(accs)
                )
            accs = list(lax.fori_loop(0, first, body, tuple(accs), unroll=2))
        for c in range(count):
            j = first + c
            diag = accs[c][c:c + 1, :]
            root = lax.rsqrt(diag)
            root = root * (1.5 - 0.5 * (diag * root) * root)
            inv[j:j + 1, :] = root
            col = accs[c] * root
            fac[pl.ds(j * ROWS + first, rows), :] = col
            for later in range(c + 1, count):
                accs[later] = accs[later] - col * col[later:later + 1, :]
    sol[48:56, :] = jnp.zeros((8, lanes), jnp.float32)
    for pan in reversed(range(7)):
        first = 8 * pan
        count = min(8, WIDTH - first)
        left = []
        for c in range(count):
            j = first + c
            val = fac[j * ROWS + WIDTH:j * ROWS + WIDTH + 1, :]
            if pan < 6:
                dot = fac[j * ROWS + first + 8:j * ROWS + ROWS, :] * sol[first + 8:ROWS, :]
                val = val - jnp.sum(dot, axis=0, keepdims=True)
            left.append(val)
        for c in reversed(range(count)):
            j = first + c
            got = left[c] * inv[j:j + 1, :]
            sol[j:j + 1, :] = got
            for early in range(c):
                row = (first + early) * ROWS + j
                left[early] = left[early] - fac[row:row + 1, :] * got


def item_solve_kernel(g_ref, out_ref, fac, inv, sol):
    solve_tile(g_ref, lambda j: g_ref[TRI + j:TRI + j + 1, :], fac, inv, sol)
    out_ref[...] = sol[:WIDTH, :]


def solve_items(packed):
    n = packed.shape[1]
    return pl.pallas_call(
        item_solve_kernel,
        out_shape=jax.ShapeDtypeStruct((WIDTH, n), jnp.float32),
        grid=(n // LANES,),
        in_specs=[pl.BlockSpec((packed.shape[0], LANES), lambda i: (0, i))],
        out_specs=pl.BlockSpec((WIDTH, LANES), lambda i: (0, i)),
        scratch_shapes=[
            pltpu.VMEM((WIDTH * ROWS, LANES), jnp.float32),
            pltpu.VMEM((ROWS, LANES), jnp.float32),
            pltpu.VMEM((ROWS, LANES), jnp.float32),
        ],
    )(packed)


PACK = 1344
FULL = 1408
SIDE = 4
HALF = PACK // 2


def cast_kernel(rate_ref, mask_ref, out_ref):
    groups = out_ref.shape[0]
    mask = mask_ref[...]
    out_ref[:, 0] = mask.astype(jnp.float32).astype(jnp.bfloat16).reshape(groups, 16, mask.shape[1])
    rated = jnp.where(mask != 0, rate_ref[...], 0.0)
    out_ref[:, 1] = rated.astype(jnp.bfloat16).reshape(groups, 16, mask.shape[1])


def cast_rows(ratings, mask):
    users, items = ratings.shape
    step = users // 8
    return pl.pallas_call(
        cast_kernel,
        out_shape=jax.ShapeDtypeStruct((users // 16, 2, 16, items), jnp.bfloat16),
        grid=(8,),
        in_specs=[pl.BlockSpec((step, items), lambda i: (i, 0))] * 2,
        out_specs=pl.BlockSpec((step // 16, 2, 16, items), lambda i: (i, 0, 0, 0)),
    )(ratings, mask)


def dot_cols(left, right):
    return lax.dot_general(left, right, (((1,), (1,)), ((), ())), preferred_element_type=jnp.float32)


def gram_kernel(
    mq, vt_ref, out_ref, rhs, vt_all, o_all, tmp, gram, rel, got, tot, flat, fin,
    v_send, v_recv, m_send, m_recv, own_sem, rel_send, rel_recv, got_send, got_recv, fin_send, fin_recv,
):
    items = vt_ref.shape[1]
    col = lax.axis_index("col")
    x = lax.rem(col, SIDE)
    y = lax.rem(col // SIDE, SIDE)
    z = col // (SIDE * SIDE)

    def turn(pos, step):
        return lax.rem(pos + step, SIDE)

    def x_peer(step):
        return {"col": col - x + turn(x, step)}

    def y_peer(step):
        return {"col": col + SIDE * (turn(y, step) - y)}

    def z_peer(step):
        return {"col": col + SIDE * SIDE * (turn(z, step) - z)}

    def send(src, dst, send_sem, recv_sem, peer):
        return pltpu.make_async_remote_copy(
            src_ref=src, dst_ref=dst, send_sem=send_sem, recv_sem=recv_sem,
            device_id=peer, device_id_type=pl.DeviceIdType.MESH,
        )

    barrier = pltpu.get_barrier_semaphore()
    peers = [x_peer(1), x_peer(2), x_peer(3), y_peer(1), y_peer(2), y_peer(3), z_peer(1), z_peer(3)]
    for peer in peers:
        pl.semaphore_signal(barrier, inc=1, device_id=peer, device_id_type=pl.DeviceIdType.MESH)
    pl.semaphore_wait(barrier, len(peers))

    v_copies = []
    for d in (1, 3, 2):
        for axis, peer in enumerate((x_peer(d), y_peer(d))):
            slot = 3 * axis + d
            v_copies.append(send(
                vt_ref, vt_all.at[:, slot * items:(slot + 1) * items],
                v_send.at[slot - 1], v_recv.at[slot - 1], peer,
            ))
    for copy in v_copies:
        copy.start()

    owners = [turn(z, 2), turn(z, 1), turn(z, 3), z]
    m_copies = []
    for k, owner in enumerate(owners):
        chunk = []
        for c, src in enumerate((mq.at[owner, :, x, 0], mq.at[owner, y, :, 1])):
            copy = pltpu.make_async_copy(src, rhs.at[k, c, :, :, :, 0:items], own_sem.at[k, c])
            chunk.append(copy)
            copy.start()
        for d in (1, 3, 2):
            for c, (src, peer) in enumerate((
                (mq.at[owner, :, turn(x, d), 0], x_peer(d)), (mq.at[owner, turn(y, d), :, 1], y_peer(d)),
            )):
                slot = 3 * c + d
                copy = send(
                    src, rhs.at[k, c, :, :, :, slot * items:(slot + 1) * items],
                    m_send.at[k, slot - 1], m_recv.at[k, slot - 1], peer,
                )
                chunk.append(copy)
                copy.start()
        m_copies.append(chunk)

    for k in range(4):
        rhs[k, 0, :, :, :, 4 * items:7 * items] = jnp.zeros((4, 2, 16, 3 * items), jnp.bfloat16)
        rhs[k, 1, :, :, :, items:4 * items] = jnp.zeros((4, 2, 16, 3 * items), jnp.bfloat16)
    tmp[1272:1280, :] = jnp.zeros((8, items), jnp.float32)
    vt_all[:, 0:items] = vt_ref[...]

    def outer_slot(slot):
        cols = pl.ds(pl.multiple_of(slot * items, items), items)
        vt = vt_all[:, cols].astype(jnp.float32)
        outer_tile(vt, tmp)
        o_all[:, cols] = tmp[...].astype(jnp.bfloat16)

    def outer_step(slot, carry):
        outer_slot(slot)
        return carry

    outer_slot(0)
    for copy in v_copies:
        copy.wait()
    lax.fori_loop(1, 7, outer_step, 0)

    def partial(k, store):
        for copy in m_copies[k]:
            copy.wait()

        def rows_step(i, carry):
            rows = pl.ds(pl.multiple_of(i * 320, 320), 320)
            store(rows, dot_cols(o_all[rows, :], rhs[k, :, :, 0].reshape(128, 7 * items)))
            return carry

        store(pl.ds(TRI, 64), dot_cols(vt_all[...], rhs[k, :, :, 1].reshape(128, 7 * items)))
        lax.fori_loop(0, 4, rows_step, 0)

    def keep(k):
        def store(rows, val):
            gram[k, rows, :] = val
        return store

    partial(0, keep(0))
    relays = [
        send(gram.at[0, 0:HALF], rel.at[0], rel_send.at[0], rel_recv.at[0], z_peer(1)),
        send(gram.at[0, HALF:PACK], rel.at[1], rel_send.at[1], rel_recv.at[1], z_peer(3)),
    ]
    for copy in relays:
        copy.start()
    partial(1, keep(1))
    relays[0].wait()
    gram[1, 0:HALF, :] = gram[1, 0:HALF, :] + rel[0]
    up = send(gram.at[1], got.at[0], got_send.at[0], got_recv.at[0], z_peer(1))
    up.start()
    partial(2, keep(2))
    relays[1].wait()
    gram[2, HALF:PACK, :] = gram[2, HALF:PACK, :] + rel[1]
    down = send(gram.at[2], got.at[1], got_send.at[1], got_recv.at[1], z_peer(3))
    down.start()

    def keep_own(rows, val):
        tot[rows, :] = val

    partial(3, keep_own)
    up.wait()
    down.wait()
    tot[PACK:FULL, :] = jnp.zeros((FULL - PACK, 128), jnp.float32)
    tot[0:PACK, :] = tot[0:PACK, :] + got[0] + got[1]
    for i in range(FULL // 128):
        flat[:, i * 128:(i + 1) * 128] = tot[i * 128:(i + 1) * 128, :].T
    f_copies = []
    for d in (2, 1, 3):
        for c, (pos, peer) in enumerate(((turn(y, d), y_peer(d)), (turn(x, d), x_peer(d)))):
            rows = pl.ds(pl.multiple_of(64 * c + 16 * pos, 16), 16)
            copy = send(flat.at[rows], fin.at[c, d - 1], fin_send.at[c, d - 1], fin_recv.at[c, d - 1], peer)
            copy.start()
            f_copies.append(copy)
    for copy in f_copies:
        copy.wait()
    for c, pos in enumerate((y, x)):
        rows = pl.ds(pl.multiple_of(64 * c + 16 * pos, 16), 16)
        out_ref[c * 16:(c + 1) * 16, :] = flat[rows, :] + fin[c, 0] + fin[c, 1] + fin[c, 2]


def gram_users(mq, vt):
    items = vt.shape[1]
    dma = pltpu.SemaphoreType.DMA
    return pl.pallas_call(
        gram_kernel,
        out_shape=jax.ShapeDtypeStruct((32, FULL), jnp.float32),
        in_specs=[pl.BlockSpec(memory_space=pl.ANY), pl.BlockSpec(memory_space=pltpu.VMEM)],
        out_specs=pl.BlockSpec(memory_space=pltpu.VMEM),
        scratch_shapes=[
            pltpu.VMEM((4, 2, 4, 2, 16, 7 * items), jnp.bfloat16),
            pltpu.VMEM((64, 7 * items), jnp.bfloat16),
            pltpu.VMEM((TRI, 7 * items), jnp.bfloat16),
            pltpu.VMEM((TRI, items), jnp.float32),
            pltpu.VMEM((3, PACK, 128), jnp.float32),
            pltpu.VMEM((2, HALF, 128), jnp.float32),
            pltpu.VMEM((2, PACK, 128), jnp.float32),
            pltpu.VMEM((FULL, 128), jnp.float32),
            pltpu.VMEM((128, FULL), jnp.float32),
            pltpu.VMEM((2, 3, 16, FULL), jnp.float32),
            dma((6,)), dma((6,)), dma((4, 6)), dma((4, 6)), dma((4, 2)),
            dma((2,)), dma((2,)), dma((2,)), dma((2,)), dma((2, 3)), dma((2, 3)),
        ],
        compiler_params=pltpu.CompilerParams(
            collective_id=0, has_side_effects=True, vmem_limit_bytes=60 * 1024 * 1024
        ),
    )(mq, vt)


def user_kernel(flat_ref, w_ref, pack_ref, gram, fac, inv, sol):
    zeros = jnp.zeros((96, 128), jnp.float32)
    for i in range(FULL // 128):
        cols = slice(i * 128, (i + 1) * 128)
        gram[cols, :] = jnp.concatenate([flat_ref[:, cols], zeros], axis=0).T
    solve_tile(gram, lambda j: gram[TRI + j:TRI + j + 1, :], fac, inv, sol)
    turned = jnp.concatenate([sol[...], jnp.zeros((72, 128), jnp.float32)], axis=0).T
    w_ref[...] = turned[:32, :WIDTH]
    lane = lax.broadcasted_iota(jnp.int32, (16, 128), 1)
    pack_ref[...] = jnp.where(lane < 64, turned[:16], pltpu.roll(turned[16:32], 64, 1)).astype(jnp.bfloat16)


def solve_users(flat):
    return pl.pallas_call(
        user_kernel,
        out_shape=(jax.ShapeDtypeStruct((32, WIDTH), jnp.float32), jax.ShapeDtypeStruct((16, 128), jnp.bfloat16)),
        scratch_shapes=[
            pltpu.VMEM((FULL, 128), jnp.float32),
            pltpu.VMEM((WIDTH * ROWS, 128), jnp.float32),
            pltpu.VMEM((ROWS, 128), jnp.float32),
            pltpu.VMEM((ROWS, 128), jnp.float32),
        ],
    )(flat)


def item_kernel(
    count, mq, pack_ref, out_ref, w_all, mqv, wt, wb, prods, tmp, part, got,
    w_send, w_recv, mq_sem, own_sem, x_send, x_recv,
):
    items = mqv.shape[-1]
    share = items // 2
    col = lax.axis_index("col")
    row = lax.axis_index("row")
    other = {"row": 1 - row}

    barrier = pltpu.get_barrier_semaphore()

    def signal_step(d, carry):
        pl.semaphore_signal(
            barrier, inc=1, device_id={"col": lax.rem(col + d, count)}, device_id_type=pl.DeviceIdType.MESH
        )
        return carry

    lax.fori_loop(1, count, signal_step, 0)
    pl.semaphore_signal(barrier, inc=1, device_id=other, device_id_type=pl.DeviceIdType.MESH)
    pl.semaphore_wait(barrier, count)

    def w_copy(d):
        return pltpu.make_async_remote_copy(
            src_ref=pack_ref, dst_ref=w_all.at[col], send_sem=w_send.at[d], recv_sem=w_recv.at[d],
            device_id={"col": lax.rem(col + d, count)}, device_id_type=pl.DeviceIdType.MESH,
        )

    def send_step(d, carry):
        w_copy(d).start()
        return carry

    lax.fori_loop(1, count, send_step, 0)
    w_own = pltpu.make_async_copy(pack_ref, w_all.at[col], own_sem.at[0])
    w_own.start()
    loads = []
    for c in range(2):
        for m in range(2):
            copy = pltpu.make_async_copy(mq.at[:, c, m], mqv.at[m, c], mq_sem.at[m, c])
            copy.start()
            loads.append(copy)
    w_own.wait()

    def wait_step(d, carry):
        w_copy(d).wait()
        return carry

    lax.fori_loop(1, count, wait_step, 0)
    for copy in loads:
        copy.wait()

    users = 16 * count
    for i in range(users // 128):
        block = w_all[8 * i:8 * i + 8].reshape(128, 128).astype(jnp.float32).T
        wt[:, i * 128:(i + 1) * 128] = block
    for c in range(2):
        wb[:, c * users:(c + 1) * users] = wt[64 * c:64 * c + 64, :].astype(jnp.bfloat16)
    step = tmp.shape[1]
    tmp[1272:1280, :] = jnp.zeros((8, step), jnp.float32)
    per = users // step

    def outer_step(i, carry):
        c = i // per
        rows = pl.ds(pl.multiple_of(64 * c, 64), 64)
        cols = pl.ds(pl.multiple_of((i - c * per) * step, step), step)
        outer_tile(wt.at[rows, cols], tmp)
        prods[:, pl.ds(pl.multiple_of(i * step, step), step)] = tmp[...].astype(jnp.bfloat16)
        return carry

    lax.fori_loop(0, 2 * per, outer_step, 0)

    def partial(half, dst):
        cols = pl.ds(pl.multiple_of(half * share, share), share)
        dst[TRI:PACK, :] = jnp.dot(
            wb[...], mqv[1, :, :, :, cols].reshape(2 * users, share), preferred_element_type=jnp.float32
        )

        def rows_step(i, carry):
            rows = pl.ds(pl.multiple_of(i * 320, 320), 320)
            dst[rows, :] = jnp.dot(
                prods[rows, :], mqv[0, :, :, :, cols].reshape(2 * users, share), preferred_element_type=jnp.float32
            )
            return carry

        lax.fori_loop(0, 4, rows_step, 0)

    partial(1 - row, part)
    swap = pltpu.make_async_remote_copy(
        src_ref=part, dst_ref=got, send_sem=x_send, recv_sem=x_recv,
        device_id=other, device_id_type=pl.DeviceIdType.MESH,
    )
    swap.start()
    partial(row, out_ref)
    swap.wait()
    out_ref[...] = out_ref[...] + got[...]


def gram_items(mq, pack, count):
    items = mq.shape[-1]
    users = 16 * count
    step = min(512, users)
    dma = pltpu.SemaphoreType.DMA
    return pl.pallas_call(
        lambda *refs: item_kernel(count, *refs),
        out_shape=jax.ShapeDtypeStruct((PACK, items // 2), jnp.float32),
        in_specs=[pl.BlockSpec(memory_space=pl.ANY), pl.BlockSpec(memory_space=pltpu.VMEM)],
        out_specs=pl.BlockSpec(memory_space=pltpu.VMEM),
        scratch_shapes=[
            pltpu.VMEM((count, 16, 128), jnp.bfloat16),
            pltpu.VMEM((2, 2, count, 16, items), jnp.bfloat16),
            pltpu.VMEM((128, users), jnp.float32),
            pltpu.VMEM((64, 2 * users), jnp.bfloat16),
            pltpu.VMEM((TRI, 2 * users), jnp.bfloat16),
            pltpu.VMEM((TRI, step), jnp.float32),
            pltpu.VMEM((PACK, items // 2), jnp.float32),
            pltpu.VMEM((PACK, items // 2), jnp.float32),
            dma((count,)), dma((count,)), dma((2, 2)), dma((1,)), dma, dma,
        ],
        compiler_params=pltpu.CompilerParams(
            collective_id=1, has_side_effects=True, vmem_limit_bytes=60 * 1024 * 1024
        ),
    )(mq, pack)


def solution(mesh):
    block_spec = P(("part", "row"), "col")
    in_specs = (block_spec, block_spec, P(("part", "col"), None))
    out_specs = (P(("part", "row", "col"), None), P(("part", "col", "row"), None))
    count = mesh.shape["col"]

    def local_als(ratings, mask, v_init):
        items = ratings.shape[1]
        mq = cast_rows(ratings, mask)
        vt = jnp.pad(v_init.T.astype(jnp.bfloat16), ((0, 64 - WIDTH), (0, 0)))
        flat = gram_users(mq.reshape(SIDE, SIDE, SIDE, 2, 2, 16, items), vt)
        w_own, w_pack = solve_users(flat)
        packed = gram_items(mq.reshape(count, 2, 2, 16, items), w_pack, count)
        v_own = solve_items(packed).T
        return w_own, v_own

    return jax.shard_map(local_als, mesh=mesh, in_specs=in_specs, out_specs=out_specs, check_vma=False)
```

time: 643 us -> 99.4 us (0.15)
  waiting for transfers between devices: 413 us -> 0 us
  blocking collectives: 148 us -> 0 us
  Pallas kernels: 19 us -> 97.7 us
  local copies, waits for them, and re-layouts: 22.9 us -> 0.63 us
  other arithmetic: 15 us -> 0.01 us
  between operations: 14.1 us -> 0.66 us
  matrix products: 10.2 us -> 0 us
    unnamed x3 -> x0, waiting for transfers between devices: 332 us -> none
    all_gather x1 -> x0, blocking collectives: 148 us -> none  [local_als(): lax.all_gather(w_own.astype(jnp.bfloat16), 'col', axis=0, tiled=True)]
    reduce_scatter x1 -> x0, waiting for transfers between devices: 80.4 us -> none  [local_als(): iown = lax.psum_scatter(both_item, 'row', scatter_dimension=1, tiled=True)]
    pallas_call x4 -> x5, Pallas kernels: 19 us -> 97.7 us  [the longest x1 50.5 us: gram_users(): pl.pallas_call(gram_kernel, out_shape=jax.ShapeDtypeStruct((32, FULL), jn...]
    unnamed x11 -> x2, local copies, waits for them, and re-layouts: 15 us -> 0.01 us
    dot_general x4 -> x0, matrix products: 10.2 us -> none  [the longest x1 6.05 us: local_als(): lax.dot_general(outer_rows(wt.astype(jnp.float32)), mask_b, contract_rows...]
    concatenate x2 -> x0, other arithmetic: 7.85 us -> none  [the longest x1 6.04 us: local_als(): both = jnp.concatenate([gram_part, rhs_part], axis=1)]
    convert_element_type x3 -> x1, other arithmetic: 6.5 us -> 0.01 us  [local_als(): vt = jnp.pad(v_init.T.astype(jnp.bfloat16), ((0, 64 - WIDTH), (0, 0)))]
  transfers between devices with their start and end apart: 2 -> 0, of which waited for: 2 -> 0; matrix products, arithmetic and copies ran while one was open for 0% -> 0% of each run, Pallas kernels for 0% -> 0%
where the time goes in v2:
time: 99.4 us; the launch traced here: 99 us
  Pallas kernels  97.7 us (98%)
    pallas_call x1, Pallas kernels, gram_users(): pl.pallas_call(gram_kernel, out_shape=jax.ShapeDtypeStruct((32, FULL), jn...  50.5 us
    pallas_call x1, Pallas kernels, gram_items(): pl.pallas_call(lambda *refs: item_kernel(count, *refs), out_shape=jax.Sha...  27.7 us
    pallas_call x1, Pallas kernels, cast_rows(): pl.pallas_call(cast_kernel, out_shape=jax.ShapeDtypeStruct((users // 16,...  7.76 us
    pallas_call x1, Pallas kernels, solve_items(): pl.pallas_call(item_solve_kernel, out_shape=jax.ShapeDtypeStruct((WIDTH,...  7.17 us
    pallas_call x1, Pallas kernels, solve_users(): pl.pallas_call(user_kernel, out_shape=(jax.ShapeDtypeStruct((32, WIDTH),...  4.54 us

profile of v2, /device:TPU:1, one launch (start us, length us, event | category | flops | bytes accessed | tf_op | source)
XLA Modules:
  0.0 99.0 jit_solution(5292849271276977824)
XLA Ops:
  0.6 0.0 copy-start
  0.6 7.8 %shard_map.50 = bf16[128,2,16,512]{3,2,1,0:T(8,128)(2,1)} custom-call(f32[2048,512]{1,0:T(8,128)} %rate_ref.1, s32[2048,512]{1,0:T(8,128)} %mask_ref.1), custom_call_target="tpu_custom_call" | custom-call | tf_op jit(solution)/shard_map/pallas_call | solution.py:122
  8.4 0.0 copy-done
  8.4 0.6 pad.4.vt_ref
  9.0 50.5 %shard_map.51.flat_ref = f32[32,1408]{1,0:T(8,128)} custom-call(bf16[4,4,4,2,2,16,512]{6,5,4,3,2,1,0:T(8,128)(2,1)} %bitcast.5, bf16[64,512]{1,0:T(8,128)(2,1)} %pad.4.vt_ref), custom_call_target="tpu_custom_call" | custom-call | tf_op jit(solution)/shard_map/pallas_call | solution.py:284
  59.6 4.5 %shard_map.52 = (f32[32,50]{1,0:T(8,128)}, bf16[16,128]{1,0:T(8,128)(2,1)}) custom-call(f32[32,1408]{1,0:T(8,128)} %shard_map.51.flat_ref), custom_call_target="tpu_custom_call" | custom-call | tf_op jit(solution)/shard_map/pallas_call | solution.py:322
  64.1 27.7 %shard_map.53.g_ref = f32[1344,256]{1,0:T(8,128)} custom-call(bf16[64,2,2,16,512]{4,3,2,1,0:T(8,128)(2,1)} %bitcast.6, bf16[16,128]{1,0:T(8,128)(2,1)} %get-tuple-element.5.refs_1_), custom_call_target="tpu_custom_call" | custom-call | tf_op jit(solution)/shard_map/pallas_call | solution.py:436
  91.8 7.2 %shard_map.54 = f32[50,256]{1,0:T(8,128)} custom-call(f32[1344,256]{1,0:T(8,128)} %shard_map.53.g_ref), custom_call_target="tpu_custom_call" | custom-call | tf_op jit(solution)/shard_map/pallas_call | solution.py:91
  (1 shorter events, 0.0 us)
Async XLA Ops:
  0.6 7.8 %copy-start = (f32[512,50]{0,1:T(8,128)S(1)}, f32[512,50]{0,1:T(8,128)}, u32[]{:S(2)}) copy-start(f32[512,50]{0,1:T(8,128)} %param.5) | copy-start | bytes 307204

commit v3 on v2

--- a/solution.py
+++ b/solution.py
@@ -108,35 +108,16 @@
 HALF = PACK // 2
 
 
-def cast_kernel(rate_ref, mask_ref, out_ref):
-    groups = out_ref.shape[0]
-    mask = mask_ref[...]
-    out_ref[:, 0] = mask.astype(jnp.float32).astype(jnp.bfloat16).reshape(groups, 16, mask.shape[1])
-    rated = jnp.where(mask != 0, rate_ref[...], 0.0)
-    out_ref[:, 1] = rated.astype(jnp.bfloat16).reshape(groups, 16, mask.shape[1])
-
-
-def cast_rows(ratings, mask):
-    users, items = ratings.shape
-    step = users // 8
-    return pl.pallas_call(
-        cast_kernel,
-        out_shape=jax.ShapeDtypeStruct((users // 16, 2, 16, items), jnp.bfloat16),
-        grid=(8,),
-        in_specs=[pl.BlockSpec((step, items), lambda i: (i, 0))] * 2,
-        out_specs=pl.BlockSpec((step // 16, 2, 16, items), lambda i: (i, 0, 0, 0)),
-    )(ratings, mask)
-
-
 def dot_cols(left, right):
     return lax.dot_general(left, right, (((1,), (1,)), ((), ())), preferred_element_type=jnp.float32)
 
 
 def gram_kernel(
-    mq, vt_ref, out_ref, rhs, vt_all, o_all, tmp, gram, rel, got, tot, flat, fin,
-    v_send, v_recv, m_send, m_recv, own_sem, rel_send, rel_recv, got_send, got_recv, fin_send, fin_recv,
+    rate_hbm, mask_hbm, v_ref, out_ref, mq_out, rate, mask, mqs, hop, rhs, vt_all, o_all, tmp, gram, rel, got, tot, flat, fin,
+    load_sem, save_sem, v_send, v_recv, m_send, m_recv, hop_send, hop_recv, fwd_send, fwd_recv, own_sem,
+    rel_send, rel_recv, got_send, got_recv, fin_send, fin_recv,
 ):
-    items = vt_ref.shape[1]
+    items = v_ref.shape[1]
     col = lax.axis_index("col")
     x = lax.rem(col, SIDE)
     y = lax.rem(col // SIDE, SIDE)
@@ -160,10 +141,26 @@
             device_id=peer, device_id_type=pl.DeviceIdType.MESH,
         )
 
+    owners = [turn(z, 2), turn(z, 1), turn(z, 3), z]
+    block = rate.shape[1]
+    loads = []
+    for k, owner in enumerate(owners):
+        rows = pl.ds(pl.multiple_of(owner * block, block), block)
+        pair = [
+            pltpu.make_async_copy(rate_hbm.at[rows], rate.at[k], load_sem.at[k, 0]),
+            pltpu.make_async_copy(mask_hbm.at[rows], mask.at[k], load_sem.at[k, 1]),
+        ]
+        for copy in pair:
+            copy.start()
+        loads.append(pair)
+
     barrier = pltpu.get_barrier_semaphore()
     peers = [x_peer(1), x_peer(2), x_peer(3), y_peer(1), y_peer(2), y_peer(3), z_peer(1), z_peer(3)]
     for peer in peers:
         pl.semaphore_signal(barrier, inc=1, device_id=peer, device_id_type=pl.DeviceIdType.MESH)
+    tmp[48:64, :] = jnp.zeros((16, items), jnp.float32)
+    tmp[0:WIDTH, :] = v_ref[...]
+    vt_all[:, 0:items] = tmp[0:64, :].astype(jnp.bfloat16)
     pl.semaphore_wait(barrier, len(peers))
 
     v_copies = []
@@ -171,56 +168,97 @@
         for axis, peer in enumerate((x_peer(d), y_peer(d))):
             slot = 3 * axis + d
             v_copies.append(send(
-                vt_ref, vt_all.at[:, slot * items:(slot + 1) * items],
+                vt_all.at[:, 0:items], vt_all.at[:, slot * items:(slot + 1) * items],
                 v_send.at[slot - 1], v_recv.at[slot - 1], peer,
             ))
     for copy in v_copies:
         copy.start()
 
-    owners = [turn(z, 2), turn(z, 1), turn(z, 3), z]
-    m_copies = []
+    def cast_chunk(k):
+        for copy in loads[k]:
+            copy.wait()
+
+        def cast_step(i, carry):
+            rows = pl.ds(pl.multiple_of(i * 128, 128), 128)
+            seen = mask[k, rows, :]
+            mqs[k, i, :, :, 0] = seen.astype(jnp.float32).astype(jnp.bfloat16).reshape(SIDE, 2, 16, items)
+            rated = jnp.where(seen != 0, rate[k, rows, :], 0.0)
+            mqs[k, i, :, :, 1] = rated.astype(jnp.bfloat16).reshape(SIDE, 2, 16, items)
+            return carry
+
+        lax.fori_loop(0, SIDE, cast_step, 0)
+
+    def axis_peer(c, step):
+        return y_peer(step) if c else x_peer(step)
+
+    def share(k, c, pos):
+        return mqs.at[k, pos, :, 1] if c else mqs.at[k, :, pos, 0]
+
+    def columns(slot):
+        return slice(slot * items, (slot + 1) * items)
+
+    m_copies, hops, passes, saves = [], [], [], []
     for k, owner in enumerate(owners):
-        chunk = []
-        for c, src in enumerate((mq.at[owner, :, x, 0], mq.at[owner, y, :, 1])):
-            copy = pltpu.make_async_copy(src, rhs.at[k, c, :, :, :, 0:items], own_sem.at[k, c])
-            chunk.append(copy)
+        saves.append(pltpu.make_async_copy(mqs.at[k], mq_out.at[owner], save_sem.at[k]))
+        m_copies.append([])
+        hops.append([])
+        passes.append([])
+        for c, pos in enumerate((x, y)):
+            m_copies[k].append(pltpu.make_async_copy(
+                share(k, c, pos), rhs.at[k, c, :, :, :, columns(0)], own_sem.at[k, c]
+            ))
+            for m, step in enumerate((1, 3)):
+                hops[k].append(send(
+                    share(k, c, turn(pos, 2)).at[:, m], hop.at[k, c, m],
+                    hop_send.at[k, c, m], hop_recv.at[k, c, m], axis_peer(c, step),
+                ))
+                m_copies[k].append(send(
+                    share(k, c, turn(pos, step)), rhs.at[k, c, :, :, :, columns(3 * c + step)],
+                    m_send.at[k, c, m], m_recv.at[k, c, m], axis_peer(c, step),
+                ))
+                passes[k].append(send(
+                    hop.at[k, c, m], rhs.at[k, c, :, m, :, columns(3 * c + 2)],
+                    fwd_send.at[k, c, m], fwd_recv.at[k, c, m], axis_peer(c, step),
+                ))
+
+    def start_chunk(k):
+        for copy in hops[k] + m_copies[k]:
             copy.start()
-        for d in (1, 3, 2):
-            for c, (src, peer) in enumerate((
-                (mq.at[owner, :, turn(x, d), 0], x_peer(d)), (mq.at[owner, turn(y, d), :, 1], y_peer(d)),
-            )):
-                slot = 3 * c + d
-                copy = send(
-                    src, rhs.at[k, c, :, :, :, slot * items:(slot + 1) * items],
-                    m_send.at[k, slot - 1], m_recv.at[k, slot - 1], peer,
-                )
-                chunk.append(copy)
-                copy.start()
-        m_copies.append(chunk)
-
+        saves[k].start()
+
+    def pass_on(k):
+        for copy, follow in zip(hops[k], passes[k]):
+            copy.wait()
+            follow.start()
+
+    cast_chunk(0)
+    start_chunk(0)
+    cast_chunk(1)
+    start_chunk(1)
+    cast_chunk(2)
+    cast_chunk(3)
     for k in range(4):
         rhs[k, 0, :, :, :, 4 * items:7 * items] = jnp.zeros((4, 2, 16, 3 * items), jnp.bfloat16)
         rhs[k, 1, :, :, :, items:4 * items] = jnp.zeros((4, 2, 16, 3 * items), jnp.bfloat16)
     tmp[1272:1280, :] = jnp.zeros((8, items), jnp.float32)
-    vt_all[:, 0:items] = vt_ref[...]
-
-    def outer_slot(slot):
+
+    def outer_step(slot, carry):
         cols = pl.ds(pl.multiple_of(slot * items, items), items)
-        vt = vt_all[:, cols].astype(jnp.float32)
-        outer_tile(vt, tmp)
+        outer_tile(vt_all[:, cols].astype(jnp.float32), tmp)
         o_all[:, cols] = tmp[...].astype(jnp.bfloat16)
-
-    def outer_step(slot, carry):
-        outer_slot(slot)
         return carry
 
-    outer_slot(0)
+    pass_on(0)
+    start_chunk(2)
     for copy in v_copies:
         copy.wait()
-    lax.fori_loop(1, 7, outer_step, 0)
+    lax.fori_loop(0, 4, outer_step, 0)
+    pass_on(1)
+    start_chunk(3)
+    lax.fori_loop(4, 7, outer_step, 0)
 
     def partial(k, store):
-        for copy in m_copies[k]:
+        for copy in m_copies[k] + passes[k]:
             copy.wait()
 
         def rows_step(i, carry):
@@ -243,11 +281,13 @@
     ]
     for copy in relays:
         copy.start()
+    pass_on(2)
     partial(1, keep(1))
     relays[0].wait()
     gram[1, 0:HALF, :] = gram[1, 0:HALF, :] + rel[0]
     up = send(gram.at[1], got.at[0], got_send.at[0], got_recv.at[0], z_peer(1))
     up.start()
+    pass_on(3)
     partial(2, keep(2))
     relays[1].wait()
     gram[2, HALF:PACK, :] = gram[2, HALF:PACK, :] + rel[1]
@@ -258,6 +298,8 @@
         tot[rows, :] = val
 
     partial(3, keep_own)
+    for copy in saves:
+        copy.wait()
     up.wait()
     down.wait()
     tot[PACK:FULL, :] = jnp.zeros((FULL - PACK, 128), jnp.float32)
@@ -278,16 +320,26 @@
         out_ref[c * 16:(c + 1) * 16, :] = flat[rows, :] + fin[c, 0] + fin[c, 1] + fin[c, 2]
 
 
-def gram_users(mq, vt):
-    items = vt.shape[1]
+def gram_users(ratings, mask, vt):
+    users, items = ratings.shape
+    block = users // SIDE
     dma = pltpu.SemaphoreType.DMA
     return pl.pallas_call(
         gram_kernel,
-        out_shape=jax.ShapeDtypeStruct((32, FULL), jnp.float32),
-        in_specs=[pl.BlockSpec(memory_space=pl.ANY), pl.BlockSpec(memory_space=pltpu.VMEM)],
-        out_specs=pl.BlockSpec(memory_space=pltpu.VMEM),
+        out_shape=(
+            jax.ShapeDtypeStruct((32, FULL), jnp.float32),
+            jax.ShapeDtypeStruct((SIDE, SIDE, SIDE, 2, 2, 16, items), jnp.bfloat16),
+        ),
+        in_specs=[
+            pl.BlockSpec(memory_space=pl.ANY), pl.BlockSpec(memory_space=pl.ANY), pl.BlockSpec(memory_space=pltpu.VMEM)
+        ],
+        out_specs=(pl.BlockSpec(memory_space=pltpu.VMEM), pl.BlockSpec(memory_space=pl.ANY)),
         scratch_shapes=[
-            pltpu.VMEM((4, 2, 4, 2, 16, 7 * items), jnp.bfloat16),
+            pltpu.VMEM((4, block, items), jnp.float32),
+            pltpu.VMEM((4, block, items), jnp.int32),
+            pltpu.VMEM((4, SIDE, SIDE, 2, 2, 16, items), jnp.bfloat16),
+            pltpu.VMEM((4, 2, 2, SIDE, 16, items), jnp.bfloat16),
+            pltpu.VMEM((4, 2, SIDE, 2, 16, 7 * items), jnp.bfloat16),
             pltpu.VMEM((64, 7 * items), jnp.bfloat16),
             pltpu.VMEM((TRI, 7 * items), jnp.bfloat16),
             pltpu.VMEM((TRI, items), jnp.float32),
@@ -297,13 +349,14 @@
             pltpu.VMEM((FULL, 128), jnp.float32),
             pltpu.VMEM((128, FULL), jnp.float32),
             pltpu.VMEM((2, 3, 16, FULL), jnp.float32),
-            dma((6,)), dma((6,)), dma((4, 6)), dma((4, 6)), dma((4, 2)),
+            dma((4, 2)), dma((4,)), dma((6,)), dma((6,)), dma((4, 2, 2)), dma((4, 2, 2)), dma((4, 2, 2)), dma((4, 2, 2)),
+            dma((4, 2, 2)), dma((4, 2, 2)), dma((4, 2)),
             dma((2,)), dma((2,)), dma((2,)), dma((2,)), dma((2, 3)), dma((2, 3)),
         ],
         compiler_params=pltpu.CompilerParams(
             collective_id=0, has_side_effects=True, vmem_limit_bytes=60 * 1024 * 1024
         ),
-    )(mq, vt)
+    )(ratings, mask, vt)
 
 
 def user_kernel(flat_ref, w_ref, pack_ref, gram, fac, inv, sol):
@@ -463,9 +516,7 @@
 
     def local_als(ratings, mask, v_init):
         items = ratings.shape[1]
-        mq = cast_rows(ratings, mask)
-        vt = jnp.pad(v_init.T.astype(jnp.bfloat16), ((0, 64 - WIDTH), (0, 0)))
-        flat = gram_users(mq.reshape(SIDE, SIDE, SIDE, 2, 2, 16, items), vt)
+        flat, mq = gram_users(ratings, mask, v_init.T)
         w_own, w_pack = solve_users(flat)
         packed = gram_items(mq.reshape(count, 2, 2, 16, items), w_pack, count)
         v_own = solve_items(packed).T

time: 99.4 us -> 95.4 us (0.960)
  Pallas kernels: 97.7 us -> 94.6 us
    pallas_call x2 -> x1, Pallas kernels: 58.3 us -> 55.8 us  [gram_users(): pl.pallas_call(gram_kernel, out_shape=(jax.ShapeDtypeStruct((32, FULL), j...]
where the time goes in v3:
time: 95.4 us; the launch traced here: 95.2 us
  Pallas kernels  94.6 us (99%)
    pallas_call x1, Pallas kernels, gram_users(): pl.pallas_call(gram_kernel, out_shape=(jax.ShapeDtypeStruct((32, FULL), j...  55.8 us
    pallas_call x1, Pallas kernels, gram_items(): pl.pallas_call(lambda *refs: item_kernel(count, *refs), out_shape=jax.Sha...  27.1 us
    pallas_call x1, Pallas kernels, solve_items(): pl.pallas_call(item_solve_kernel, out_shape=jax.ShapeDtypeStruct((WIDTH,...  7.17 us
    pallas_call x1, Pallas kernels, solve_users(): pl.pallas_call(user_kernel, out_shape=(jax.ShapeDtypeStruct((32, WIDTH),...  4.54 us

profile of v3, /device:TPU:1, one launch (start us, length us, event | category | flops | bytes accessed | tf_op | source)
XLA Modules:
  0.0 95.2 jit_solution(3934017467167297922)
XLA Ops:
  0.6 55.8 %shard_map.50 = (f32[32,1408]{1,0:T(8,128)}, bf16[4,4,4,2,2,16,512]{6,5,4,3,2,1,0:T(8,128)(2,1)}) custom-call(f32[2048,512]{1,0:T(8,128)} %rate_hbm.1, s32[2048,512]{1,0:T(8,128)} %mask_hbm.1, f32[50,512]{1,0:T(8,128)} %bitcast.4), custom_call_target="tpu_custom_call" | custom-call | tf_op jit(solution)/shard_map/pallas_call | solution.py:327
  56.4 4.5 %shard_map.51 = (f32[32,50]{1,0:T(8,128)}, bf16[16,128]{1,0:T(8,128)(2,1)}) custom-call(f32[32,1408]{1,0:T(8,128)} %get-tuple-element.6.flat_ref), custom_call_target="tpu_custom_call" | custom-call | tf_op jit(solution)/shard_map/pallas_call | solution.py:375
  61.0 27.1 %shard_map.52.g_ref = f32[1344,256]{1,0:T(8,128)} custom-call(bf16[64,2,2,16,512]{4,3,2,1,0:T(8,128)(2,1)} %bitcast.3, bf16[16,128]{1,0:T(8,128)(2,1)} %get-tuple-element.9.refs_1_), custom_call_target="tpu_custom_call" | custom-call | tf_op jit(solution)/shard_map/pallas_call | solution.py:489
  88.1 7.2 %shard_map.53 = f32[50,256]{1,0:T(8,128)} custom-call(f32[1344,256]{1,0:T(8,128)} %shard_map.52.g_ref), custom_call_target="tpu_custom_call" | custom-call | tf_op jit(solution)/shard_map/pallas_call | solution.py:91

commit v4 on v1

v4 whole, which is shorter than its diff:
```python
import jax
import jax.numpy as jnp
from jax import lax
from jax.experimental import pallas as pl
from jax.experimental.pallas import tpu as pltpu
from jax.sharding import PartitionSpec as P

RIDGE_WEIGHT = 0.05
WIDTH = 50
ROWS = 56
TRI = 1280
LANES = 128


def tri_off(j):
    return j * WIDTH - j * (j - 1) // 2


def outer_tile(vt, dst):
    lanes = vt.shape[1]
    for j in range(WIDTH):
        rows = WIDTH - j
        dst[tri_off(j):tri_off(j) + rows, :] = vt[j:WIDTH, :] * vt[j:j + 1, :]


def solve_tile(g_ref, rhs, fac, inv, sol):
    lanes = fac.shape[1]
    for pan in range(7):
        first = 8 * pan
        rows = ROWS - first
        count = min(8, WIDTH - first)
        ids = lax.broadcasted_iota(jnp.int32, (rows, lanes), 0)
        accs = []
        for c in range(count):
            j = first + c
            start = tri_off(j) - c
            if j < WIDTH - 1:
                raw = g_ref[start:start + rows, :]
            else:
                raw = jnp.broadcast_to(g_ref[tri_off(j):tri_off(j) + 1, :], (rows, lanes))
            col = jnp.where(ids < WIDTH - first, raw, 0.0)
            col = jnp.where(ids == c, col + RIDGE_WEIGHT, col)
            col = jnp.where(ids == WIDTH - first, rhs(j), col)
            accs.append(col)
        if pan:
            def body(k, accs):
                base = pl.multiple_of(k * ROWS, 8)
                left = fac[pl.ds(base + first, rows), :]
                return tuple(
                    acc - left * fac[pl.ds(base + first + c, 1), :] for c, acc in enumerate(accs)
                )
            accs = list(lax.fori_loop(0, first, body, tuple(accs), unroll=2))
        for c in range(count):
            j = first + c
            diag = accs[c][c:c + 1, :]
            root = lax.rsqrt(diag)
            root = root * (1.5 - 0.5 * (diag * root) * root)
            inv[j:j + 1, :] = root
            col = accs[c] * root
            fac[pl.ds(j * ROWS + first, rows), :] = col
            for later in range(c + 1, count):
                accs[later] = accs[later] - col * col[later:later + 1, :]
    sol[48:56, :] = jnp.zeros((8, lanes), jnp.float32)
    for pan in reversed(range(7)):
        first = 8 * pan
        count = min(8, WIDTH - first)
        left = []
        for c in range(count):
            j = first + c
            val = fac[j * ROWS + WIDTH:j * ROWS + WIDTH + 1, :]
            if pan < 6:
                dot = fac[j * ROWS + first + 8:j * ROWS + ROWS, :] * sol[first + 8:ROWS, :]
                val = val - jnp.sum(dot, axis=0, keepdims=True)
            left.append(val)
        for c in reversed(range(count)):
            j = first + c
            got = left[c] * inv[j:j + 1, :]
            sol[j:j + 1, :] = got
            for early in range(c):
                row = (first + early) * ROWS + j
                left[early] = left[early] - fac[row:row + 1, :] * got


def item_solve_kernel(g_ref, out_ref, fac, inv, sol):
    solve_tile(g_ref, lambda j: g_ref[TRI + j:TRI + j + 1, :], fac, inv, sol)
    out_ref[...] = sol[:WIDTH, :]


def solve_items(packed):
    n = packed.shape[1]
    return pl.pallas_call(
        item_solve_kernel,
        out_shape=jax.ShapeDtypeStruct((WIDTH, n), jnp.float32),
        grid=(n // LANES,),
        in_specs=[pl.BlockSpec((packed.shape[0], LANES), lambda i: (0, i))],
        out_specs=pl.BlockSpec((WIDTH, LANES), lambda i: (0, i)),
        scratch_shapes=[
            pltpu.VMEM((WIDTH * ROWS, LANES), jnp.float32),
            pltpu.VMEM((ROWS, LANES), jnp.float32),
            pltpu.VMEM((ROWS, LANES), jnp.float32),
        ],
    )(packed)


PACK = 1344
FULL = 1408
SIDE = 4
HALF = PACK // 2


def dot_cols(left, right):
    return lax.dot_general(left, right, (((1,), (1,)), ((), ())), preferred_element_type=jnp.float32)


def als_kernel(
    rate_hbm, mask_hbm, v_ref, w_ref, item_ref,
    rate, mask, mqs, hop, rhs, vt_all, o_all, tmp, gram, unit, rel, got, tot, flat, fin,
    fac, inv, sol, pack, w_all, wt, wb, part, swap_got,
    load_sem, v_send, v_recv, m_send, m_recv, hop_send, hop_recv, fwd_send, fwd_recv, own_sem,
    rel_send, rel_recv, got_send, got_recv, fin_send, fin_recv, w_send, w_recv, w_sem, x_send, x_recv, y_in, z_in,
):
    items = v_ref.shape[1]
    count = w_all.shape[0]
    col = lax.axis_index("col")
    row = lax.axis_index("row")
    other = {"row": 1 - row}
    x = lax.rem(col, SIDE)
    y = lax.rem(col // SIDE, SIDE)
    z = col // (SIDE * SIDE)

    def turn(pos, step):
        return lax.rem(pos + step, SIDE)

    def x_peer(step):
        return {"col": col - x + turn(x, step)}

    def y_peer(step):
        return {"col": col + SIDE * (turn(y, step) - y)}

    def z_peer(step):
        return {"col": col + SIDE * SIDE * (turn(z, step) - z)}

    def send(src, dst, send_sem, recv_sem, peer):
        return pltpu.make_async_remote_copy(
            src_ref=src, dst_ref=dst, send_sem=send_sem, recv_sem=recv_sem,
            device_id=peer, device_id_type=pl.DeviceIdType.MESH,
        )

    def signal(sem, peer):
        pl.semaphore_signal(sem, inc=1, device_id=peer, device_id_type=pl.DeviceIdType.MESH)

    barrier = pltpu.get_barrier_semaphore()
    peers = [peer(step) for step in (1, 2, 3) for peer in (x_peer, y_peer, z_peer)] + [other]
    for peer in peers:
        signal(barrier, peer)

    owners = [turn(z, 2), turn(z, 1), turn(z, 3), z]
    block = rate.shape[1]
    loads = []
    for k, owner in enumerate(owners):
        rows = pl.ds(pl.multiple_of(owner * block, block), block)
        pair = [
            pltpu.make_async_copy(rate_hbm.at[rows], rate.at[k], load_sem.at[k, 0]),
            pltpu.make_async_copy(mask_hbm.at[rows], mask.at[k], load_sem.at[k, 1]),
        ]
        for copy in pair:
            copy.start()
        loads.append(pair)

    def cast_chunk(k):
        for copy in loads[k]:
            copy.wait()

        def cast_step(i, carry):
            rows = pl.ds(pl.multiple_of(i * 128, 128), 128)
            seen = mask[k, rows, :]
            mqs[k, i, :, :, 0] = seen.astype(jnp.float32).astype(jnp.bfloat16).reshape(SIDE, 2, 16, items)
            rated = jnp.where(seen != 0, rate[k, rows, :], 0.0)
            mqs[k, i, :, :, 1] = rated.astype(jnp.bfloat16).reshape(SIDE, 2, 16, items)
            return carry

        lax.fori_loop(0, SIDE, cast_step, 0)

    def axis_peer(c, step):
        return y_peer(step) if c else x_peer(step)

    def share(s, c, pos):
        return mqs.at[(0, 2, 1, 3)[s], pos, :, 1] if c else mqs.at[s, :, pos, 0]

    def columns(slot):
        return slice(slot * items, (slot + 1) * items)

    m_copies, hops, passes = [], [], []
    for s in range(4):
        m_copies.append([])
        hops.append([])
        passes.append([])
        for c, pos in enumerate((x, y)):
            for m, step in enumerate((1, 3)):
                hops[s].append(send(
                    share(s, c, turn(pos, 2)).at[:, m], hop.at[s, c, m],
                    hop_send.at[s, c, m], hop_recv.at[s, c, m], axis_peer(c, step),
                ))
                m_copies[s].append(send(
                    share(s, c, turn(pos, step)), rhs.at[s, c, :, :, :, columns(3 * c + step)],
                    m_send.at[s, c, m], m_recv.at[s, c, m], axis_peer(c, step),
                ))
                passes[s].append(send(
                    hop.at[s, c, m], rhs.at[s, c, :, m, :, columns(3 * c + 2)],
                    fwd_send.at[s, c, m], fwd_recv.at[s, c, m], axis_peer(c, step),
                ))
            m_copies[s].append(pltpu.make_async_copy(
                share(s, c, pos), rhs.at[s, c, :, :, :, columns(0)], own_sem.at[s, c]
            ))

    def start_stage(s):
        for copy in hops[s] + m_copies[s]:
            copy.start()

    def pass_on(s):
        for copy, follow in zip(hops[s], passes[s]):
            copy.wait()
            follow.start()

    tmp[48:64, :] = jnp.zeros((16, items), jnp.float32)
    tmp[0:WIDTH, :] = v_ref[...]
    vt_all[:, 0:items] = tmp[0:64, :].astype(jnp.bfloat16)
    cast_chunk(0)
    pl.semaphore_wait(barrier, len(peers))
    start_stage(0)
    v_copies = []
    for d in (1, 3, 2):
        for axis in range(2):
            slot = 3 * axis + d
            v_copies.append(send(
                vt_all.at[:, columns(0)], vt_all.at[:, columns(slot)],
                v_send.at[slot - 1], v_recv.at[slot - 1], axis_peer(axis, d),
            ))
    for copy in v_copies:
        copy.start()
    for step in (1, 2, 3):
        signal(y_in, y_peer(step))
    for k in range(1, 4):
        cast_chunk(k)
    for s in range(4):
        rhs[s, 0, :, :, :, 4 * items:7 * items] = jnp.zeros((4, 2, 16, 3 * items), jnp.bfloat16)
        rhs[s, 1, :, :, :, items:4 * items] = jnp.zeros((4, 2, 16, 3 * items), jnp.bfloat16)
    tmp[1272:1280, :] = jnp.zeros((8, items), jnp.float32)

    def outer_step(slot, carry):
        cols = pl.ds(pl.multiple_of(slot * items, items), items)
        outer_tile(vt_all[:, cols].astype(jnp.float32), tmp)
        o_all[:, cols] = tmp[...].astype(jnp.bfloat16)
        return carry

    lax.fori_loop(0, 1, outer_step, 0)
    pass_on(0)
    start_stage(1)
    pl.semaphore_wait(y_in, 3)
    for step in (1, 2, 3):
        signal(z_in, z_peer(step))
    for copy in v_copies:
        copy.wait()
    lax.fori_loop(1, 7, outer_step, 0)

    def partial(s, dst):
        for copy in m_copies[s] + passes[s]:
            copy.wait()

        def rows_step(i, carry):
            rows = pl.ds(pl.multiple_of(i * 320, 320), 320)
            dst[rows, :] = dot_cols(o_all[rows, :], rhs[s, :, :, 0].reshape(128, 7 * items))
            return carry

        dst[TRI:PACK, :] = dot_cols(vt_all[...], rhs[s, :, :, 1].reshape(128, 7 * items))
        lax.fori_loop(0, 4, rows_step, 0)

    low = lax.broadcasted_iota(jnp.int32, (HALF, 128), 1) < 64

    def pack_units(s):
        top, bottom = gram[0:HALF, :], gram[HALF:PACK, :]
        unit[s, 0] = jnp.where(low, top, pltpu.roll(bottom, 64, 1))
        unit[s, 1] = jnp.where(low, pltpu.roll(top, 64, 1), bottom)

    pieces = (slice(0, HALF // 2), slice(HALF // 2, HALF))
    ways = (1, 3)
    partial(0, gram)
    pack_units(0)
    relays = [[
        send(unit.at[0, c, rows], rel.at[c, rows], rel_send.at[c, p], rel_recv.at[c, p], z_peer(ways[c]))
        for c in range(2)
    ] for p, rows in enumerate(pieces)]
    for piece in relays:
        for copy in piece:
            copy.start()
    pass_on(1)
    start_stage(2)
    partial(1, gram)
    pack_units(1)
    z_copies = []
    pass_on(2)
    start_stage(3)
    for p, rows in enumerate(pieces):
        for c in range(2):
            relays[p][c].wait()
            unit[1, c, rows, :] = unit[1, c, rows, :] + rel[c, rows, :]
            copy = send(
                unit.at[1, c, rows], got.at[0, c, rows], got_send.at[0, c, p], got_recv.at[0, c, p], z_peer(ways[c])
            )
            copy.start()
            z_copies.append(copy)
    pass_on(3)
    partial(2, gram)
    pack_units(2)
    for c in range(2):
        copy = send(
            unit.at[2, c], got.at[1, c], got_send.at[1, c, 0], got_recv.at[1, c, 0], z_peer(ways[1 - c])
        )
        copy.start()
        z_copies.append(copy)
    partial(3, tot)
    tot[PACK:FULL, :] = jnp.zeros((FULL - PACK, 128), jnp.float32)
    for copy in z_copies:
        copy.wait()
    sum_a = got[0, 0] + got[1, 0]
    sum_b = got[0, 1] + got[1, 1]
    tot[0:HALF, :] = tot[0:HALF, :] + jnp.where(low, sum_a, pltpu.roll(sum_b, 64, 1))
    tot[HALF:PACK, :] = tot[HALF:PACK, :] + jnp.where(low, pltpu.roll(sum_a, 64, 1), sum_b)
    for i in range(FULL // 128):
        flat[:, i * 128:(i + 1) * 128] = tot[i * 128:(i + 1) * 128, :].T
    f_copies = []
    for d in (2, 1, 3):
        for c, pos in enumerate((y, x)):
            rows = pl.ds(pl.multiple_of(64 * c + 16 * turn(pos, d), 16), 16)
            copy = send(
                flat.at[rows], fin.at[c, d - 1], fin_send.at[c, d - 1], fin_recv.at[c, d - 1], axis_peer(1 - c, d)
            )
            copy.start()
            f_copies.append(copy)
    pl.semaphore_wait(z_in, 3)
    for copy in f_copies:
        copy.wait()

    zeros = jnp.zeros((96, 128), jnp.float32)
    for i in range(FULL // 128):
        cols = slice(i * 128, (i + 1) * 128)
        mine = [zeros]
        for c, pos in ((1, x), (0, y)):
            rows = pl.ds(pl.multiple_of(64 * c + 16 * pos, 16), 16)
            mine.insert(0, flat[rows, cols] + fin[c, 0, :, cols] + fin[c, 1, :, cols] + fin[c, 2, :, cols])
        tot[cols, :] = jnp.concatenate(mine, axis=0).T
    solve_tile(tot, lambda j: tot[TRI + j:TRI + j + 1, :], fac, inv, sol)
    turned = jnp.concatenate([sol[...], jnp.zeros((72, 128), jnp.float32)], axis=0).T
    lane = lax.broadcasted_iota(jnp.int32, (16, 128), 1)
    pack[...] = jnp.where(lane < 64, turned[:16], pltpu.roll(turned[16:32], 64, 1)).astype(jnp.bfloat16)

    def w_copy(d):
        return send(pack, w_all.at[col], w_send.at[d], w_recv.at[d], {"col": lax.rem(col + d, count)})

    def send_step(d, carry):
        w_copy(d).start()
        return carry

    def wait_step(d, carry):
        w_copy(d).wait()
        return carry

    lax.fori_loop(1, count, send_step, 0)
    w_own = pltpu.make_async_copy(pack, w_all.at[col], w_sem)
    w_own.start()
    w_ref[...] = turned[:32, :WIDTH]
    w_own.wait()
    lax.fori_loop(1, count, wait_step, 0)

    users = 16 * count
    for i in range(users // 128):
        wt[:, i * 128:(i + 1) * 128] = w_all[8 * i:8 * i + 8].reshape(128, 128).astype(jnp.float32).T
    step = users // SIDE
    tall = tmp.at[:, 0:step]
    tall[1272:1280, :] = jnp.zeros((8, step), jnp.float32)

    def w_step(i, carry):
        c = i // SIDE
        k = i - c * SIDE
        owner = turn(z, 2 - k + (k // 2) * (2 * k - 1))
        rows = pl.ds(pl.multiple_of(64 * c, 64), 64)
        vals = wt[rows, pl.ds(pl.multiple_of(owner * step, step), step)]
        cols = pl.ds(pl.multiple_of(i * step, step), step)
        wb[:, cols] = vals.astype(jnp.bfloat16)
        outer_tile(vals, tall)
        o_all[:, cols] = tall[...].astype(jnp.bfloat16)
        return carry

    lax.fori_loop(0, 2 * SIDE, w_step, 0)
    half = items // 2

    def item_partial(side, dst):
        cols = pl.ds(pl.multiple_of(side * half, half), half)

        def both(left, m):
            total = None
            for c in range(2):
                right = mqs[:, :, :, c, m, :, cols].reshape(users, half)
                term = jnp.dot(left(c), right, preferred_element_type=jnp.float32)
                total = term if total is None else total + term
            return total

        dst[TRI:PACK, :] = both(lambda c: wb[:, c * users:(c + 1) * users], 1)

        def rows_step(i, carry):
            rows = pl.ds(pl.multiple_of(i * 320, 320), 320)
            dst[rows, :] = both(lambda c: o_all[rows, c * users:(c + 1) * users], 0)
            return carry

        lax.fori_loop(0, 4, rows_step, 0)

    item_partial(1 - row, part)
    swap = send(part, swap_got, x_send, x_recv, other)
    swap.start()
    item_partial(row, item_ref)
    swap.wait()
    item_ref[...] = item_ref[...] + swap_got[...]


def half_steps(ratings, mask, vt, count):
    users, items = ratings.shape
    block = users // SIDE
    dma = pltpu.SemaphoreType.DMA
    any_spec = pl.BlockSpec(memory_space=pl.ANY)
    vmem_spec = pl.BlockSpec(memory_space=pltpu.VMEM)
    f32, bf16 = jnp.float32, jnp.bfloat16
    return pl.pallas_call(
        als_kernel,
        out_shape=(
            jax.ShapeDtypeStruct((32, WIDTH), f32),
            jax.ShapeDtypeStruct((PACK, items // 2), f32),
        ),
        in_specs=[any_spec, any_spec, vmem_spec],
        out_specs=(vmem_spec, vmem_spec),
        scratch_shapes=[
            pltpu.VMEM((4, block, items), f32),
            pltpu.VMEM((4, block, items), jnp.int32),
            pltpu.VMEM((4, SIDE, SIDE, 2, 2, 16, items), bf16),
            pltpu.VMEM((4, 2, 2, SIDE, 16, items), bf16),
            pltpu.VMEM((4, 2, SIDE, 2, 16, 7 * items), bf16),
            pltpu.VMEM((64, 7 * items), bf16),
            pltpu.VMEM((TRI, 7 * items), bf16),
            pltpu.VMEM((TRI, items), f32),
            pltpu.VMEM((PACK, 128), f32),
            pltpu.VMEM((3, 2, HALF, 128), f32),
            pltpu.VMEM((2, HALF, 128), f32),
            pltpu.VMEM((2, 2, HALF, 128), f32),
            pltpu.VMEM((FULL, 128), f32),
            pltpu.VMEM((128, FULL), f32),
            pltpu.VMEM((2, 3, 16, FULL), f32),
            pltpu.VMEM((WIDTH * ROWS, 128), f32),
            pltpu.VMEM((ROWS, 128), f32),
            pltpu.VMEM((ROWS, 128), f32),
            pltpu.VMEM((16, 128), bf16),
            pltpu.VMEM((count, 16, 128), bf16),
            pltpu.VMEM((128, 16 * count), f32),
            pltpu.VMEM((64, 32 * count), bf16),
            pltpu.VMEM((PACK, items // 2), f32),
            pltpu.VMEM((PACK, items // 2), f32),
            dma((4, 2)), dma((6,)), dma((6,)), dma((4, 2, 2)), dma((4, 2, 2)), dma((4, 2, 2)), dma((4, 2, 2)),
            dma((4, 2, 2)), dma((4, 2, 2)), dma((4, 2)),
            dma((2, 2)), dma((2, 2)), dma((2, 2, 2)), dma((2, 2, 2)), dma((2, 3)), dma((2, 3)),
            dma((count,)), dma((count,)), dma, dma, dma,
            pltpu.SemaphoreType.REGULAR, pltpu.SemaphoreType.REGULAR,
        ],
        compiler_params=pltpu.CompilerParams(
            collective_id=0, has_side_effects=True, vmem_limit_bytes=60 * 1024 * 1024
        ),
    )(ratings, mask, vt)


def solution(mesh):
    block_spec = P(("part", "row"), "col")
    in_specs = (block_spec, block_spec, P(("part", "col"), None))
    out_specs = (P(("part", "row", "col"), None), P(("part", "col", "row"), None))
    count = mesh.shape["col"]

    def local_als(ratings, mask, v_init):
        w_own, packed = half_steps(ratings, mask, v_init.T, count)
        v_own = solve_items(packed).T
        return w_own, v_own

    return jax.shard_map(local_als, mesh=mesh, in_specs=in_specs, out_specs=out_specs, check_vma=False)
```

time: 643 us -> 84.5 us (0.13)
  waiting for transfers between devices: 413 us -> 0 us
  blocking collectives: 148 us -> 0 us
  Pallas kernels: 19 us -> 82.3 us
  local copies, waits for them, and re-layouts: 22.9 us -> 1.32 us
  other arithmetic: 15 us -> 0 us
  between operations: 14.1 us -> 0.64 us
  matrix products: 10.2 us -> 0 us
    unnamed x3 -> x0, waiting for transfers between devices: 332 us -> none
    all_gather x1 -> x0, blocking collectives: 148 us -> none  [local_als(): lax.all_gather(w_own.astype(jnp.bfloat16), 'col', axis=0, tiled=True)]
    reduce_scatter x1 -> x0, waiting for transfers between devices: 80.4 us -> none  [local_als(): iown = lax.psum_scatter(both_item, 'row', scatter_dimension=1, tiled=True)]
    pallas_call x4 -> x2, Pallas kernels: 19 us -> 82.3 us  [the longest x1 75.1 us: half_steps(): pl.pallas_call(als_kernel, out_shape=(jax.ShapeDtypeStruct((32, WIDTH), f...]
    unnamed x11 -> x1, local copies, waits for them, and re-layouts: 15 us -> 1.32 us
    dot_general x4 -> x0, matrix products: 10.2 us -> none  [the longest x1 6.05 us: local_als(): lax.dot_general(outer_rows(wt.astype(jnp.float32)), mask_b, contract_rows...]
    concatenate x2 -> x0, other arithmetic: 7.85 us -> none  [the longest x1 6.04 us: local_als(): both = jnp.concatenate([gram_part, rhs_part], axis=1)]
    convert_element_type x3 -> x0, other arithmetic: 6.5 us -> none  [the longest x1 4.73 us: local_als(): rated_b = jnp.where(mask != 0, ratings, 0.0).astype(jnp.bfloat16)]
  transfers between devices with their start and end apart: 2 -> 0, of which waited for: 2 -> 0; matrix products, arithmetic and copies ran while one was open for 0% -> 0% of each run, Pallas kernels for 0% -> 0%
where the time goes in v4:
time: 84.5 us; the launch traced here: 84.3 us
  Pallas kernels  82.3 us (97%)
  local copies, waits for them, and re-layouts  1.32 us (2%)
    pallas_call x1, Pallas kernels, half_steps(): pl.pallas_call(als_kernel, out_shape=(jax.ShapeDtypeStruct((32, WIDTH), f...  75.1 us
    pallas_call x1, Pallas kernels, solve_items(): pl.pallas_call(item_solve_kernel, out_shape=jax.ShapeDtypeStruct((WIDTH,...  7.17 us

profile of v4, /device:TPU:1, one launch (start us, length us, event | category | flops | bytes accessed | tf_op | source)
XLA Modules:
  0.0 84.3 jit_solution(15155750740121365176)
XLA Ops:
  0.6 75.1 %shard_map.50 = (f32[32,50]{1,0:T(8,128)}, f32[1344,256]{1,0:T(8,128)}) custom-call(f32[2048,512]{1,0:T(8,128)} %rate_hbm.1, s32[2048,512]{1,0:T(8,128)} %mask_hbm.1, f32[50,512]{1,0:T(8,128)} %bitcast.2), custom_call_target="tpu_custom_call" | custom-call | tf_op jit(solution)/shard_map/pallas_call | solution.py:432
  75.8 7.2 %shard_map.51 = f32[50,256]{1,0:T(8,128)} custom-call(f32[1344,256]{1,0:T(8,128)} %get-tuple-element.5.g_ref), custom_call_target="tpu_custom_call" | custom-call | tf_op jit(solution)/shard_map/pallas_call | solution.py:91
  83.0 1.3 %copy.6 = f32[32,50]{1,0:T(8,128)} copy(f32[32,50]{1,0:T(8,128)} %get-tuple-element.8) | data formatting | bytes 12800

commit v5 on v4

--- a/solution.py
+++ b/solution.py
@@ -81,31 +81,34 @@
                 left[early] = left[early] - fac[row:row + 1, :] * got
 
 
-def item_solve_kernel(g_ref, out_ref, fac, inv, sol):
+def item_solve_kernel(g_ref, w_ref, out_ref, w_out, fac, inv, sol):
+    w_out[...] = w_ref[...]
     solve_tile(g_ref, lambda j: g_ref[TRI + j:TRI + j + 1, :], fac, inv, sol)
     out_ref[...] = sol[:WIDTH, :]
 
 
-def solve_items(packed):
+def solve_items(packed, w_own):
     n = packed.shape[1]
+    w_spec = pl.BlockSpec(w_own.shape, lambda i: (0, 0))
     return pl.pallas_call(
         item_solve_kernel,
-        out_shape=jax.ShapeDtypeStruct((WIDTH, n), jnp.float32),
+        out_shape=(jax.ShapeDtypeStruct((WIDTH, n), jnp.float32), jax.ShapeDtypeStruct(w_own.shape, jnp.float32)),
         grid=(n // LANES,),
-        in_specs=[pl.BlockSpec((packed.shape[0], LANES), lambda i: (0, i))],
-        out_specs=pl.BlockSpec((WIDTH, LANES), lambda i: (0, i)),
+        in_specs=[pl.BlockSpec((packed.shape[0], LANES), lambda i: (0, i)), w_spec],
+        out_specs=(pl.BlockSpec((WIDTH, LANES), lambda i: (0, i)), w_spec),
         scratch_shapes=[
             pltpu.VMEM((WIDTH * ROWS, LANES), jnp.float32),
             pltpu.VMEM((ROWS, LANES), jnp.float32),
             pltpu.VMEM((ROWS, LANES), jnp.float32),
         ],
-    )(packed)
+    )(packed, w_own)
 
 
 PACK = 1344
 FULL = 1408
 SIDE = 4
 HALF = PACK // 2
+CUT = 384
 
 
 def dot_cols(left, right):
@@ -113,13 +116,13 @@
 
 
 def als_kernel(
-    rate_hbm, mask_hbm, v_ref, w_ref, item_ref,
-    rate, mask, mqs, hop, rhs, vt_all, o_all, tmp, gram, unit, rel, got, tot, flat, fin,
-    fac, inv, sol, pack, w_all, wt, wb, part, swap_got,
-    load_sem, v_send, v_recv, m_send, m_recv, hop_send, hop_recv, fwd_send, fwd_recv, own_sem,
-    rel_send, rel_recv, got_send, got_recv, fin_send, fin_recv, w_send, w_recv, w_sem, x_send, x_recv, y_in, z_in,
+    rate_hbm, mask_hbm, v_hbm, w_hbm, item_hbm,
+    rate, mask, v_raw, mqs, hop, rhs, vt_all, o_all, tmp, gram, unit, rel, got, tot, acc, flat, fin,
+    fac, inv, sol, w_new, pack, w_all, wt, wb, part, swap_got, item_sum,
+    v_sem, load_sem, v_send, v_recv, m_send, m_recv, hop_send, hop_recv, fwd_send, fwd_recv, own_sem,
+    rel_send, rel_recv, got_send, got_recv, fin_send, fin_recv, w_send, w_recv, w_sem, x_send, x_recv, out_sem, y_in, z_in,
 ):
-    items = v_ref.shape[1]
+    items = v_raw.shape[1]
     count = w_all.shape[0]
     col = lax.axis_index("col")
     row = lax.axis_index("row")
@@ -156,6 +159,7 @@
 
     owners = [turn(z, 2), turn(z, 1), turn(z, 3), z]
     block = rate.shape[1]
+    v_load = pltpu.make_async_copy(v_hbm, v_raw, v_sem)
     loads = []
     for k, owner in enumerate(owners):
         rows = pl.ds(pl.multiple_of(owner * block, block), block)
@@ -166,6 +170,8 @@
         for copy in pair:
             copy.start()
         loads.append(pair)
+        if k == 0:
+            v_load.start()
 
     def cast_chunk(k):
         for copy in loads[k]:
@@ -223,9 +229,10 @@
             follow.start()
 
     tmp[48:64, :] = jnp.zeros((16, items), jnp.float32)
-    tmp[0:WIDTH, :] = v_ref[...]
+    cast_chunk(0)
+    v_load.wait()
+    tmp[0:WIDTH, :] = v_raw[...]
     vt_all[:, 0:items] = tmp[0:64, :].astype(jnp.bfloat16)
-    cast_chunk(0)
     pl.semaphore_wait(barrier, len(peers))
     start_stage(0)
     v_copies = []
@@ -282,7 +289,7 @@
         unit[s, 0] = jnp.where(low, top, pltpu.roll(bottom, 64, 1))
         unit[s, 1] = jnp.where(low, pltpu.roll(top, 64, 1), bottom)
 
-    pieces = (slice(0, HALF // 2), slice(HALF // 2, HALF))
+    pieces = (slice(0, CUT), slice(CUT, HALF))
     ways = (1, 3)
     partial(0, gram)
     pack_units(0)
@@ -312,32 +319,43 @@
     pass_on(3)
     partial(2, gram)
     pack_units(2)
-    for c in range(2):
-        copy = send(
-            unit.at[2, c], got.at[1, c], got_send.at[1, c, 0], got_recv.at[1, c, 0], z_peer(ways[1 - c])
-        )
-        copy.start()
-        z_copies.append(copy)
+    last = [[
+        send(unit.at[2, c, rows], got.at[1, c, rows], got_send.at[1, c, p], got_recv.at[1, c, p], z_peer(ways[1 - c]))
+        for c in range(2)
+    ] for p, rows in enumerate(pieces)]
+    for piece in last:
+        for copy in piece:
+            copy.start()
     partial(3, tot)
-    tot[PACK:FULL, :] = jnp.zeros((FULL - PACK, 128), jnp.float32)
+    acc[PACK:FULL, :] = jnp.zeros((FULL - PACK, 128), jnp.float32)
     for copy in z_copies:
         copy.wait()
-    sum_a = got[0, 0] + got[1, 0]
-    sum_b = got[0, 1] + got[1, 1]
-    tot[0:HALF, :] = tot[0:HALF, :] + jnp.where(low, sum_a, pltpu.roll(sum_b, 64, 1))
-    tot[HALF:PACK, :] = tot[HALF:PACK, :] + jnp.where(low, pltpu.roll(sum_a, 64, 1), sum_b)
-    for i in range(FULL // 128):
-        flat[:, i * 128:(i + 1) * 128] = tot[i * 128:(i + 1) * 128, :].T
+    pl.semaphore_wait(z_in, 3)
     f_copies = []
-    for d in (2, 1, 3):
-        for c, pos in enumerate((y, x)):
-            rows = pl.ds(pl.multiple_of(64 * c + 16 * turn(pos, d), 16), 16)
-            copy = send(
-                flat.at[rows], fin.at[c, d - 1], fin_send.at[c, d - 1], fin_recv.at[c, d - 1], axis_peer(1 - c, d)
-            )
-            copy.start()
-            f_copies.append(copy)
-    pl.semaphore_wait(z_in, 3)
+    for p, rows in enumerate(pieces):
+        size = rows.stop - rows.start
+        for copy in last[p]:
+            copy.wait()
+        sum_a = got[0, 0, rows] + got[1, 0, rows]
+        sum_b = got[0, 1, rows] + got[1, 1, rows]
+        here = low[:size]
+        at = 2 * rows.start
+        acc[at:at + size, :] = tot[rows, :] + jnp.where(here, sum_a, pltpu.roll(sum_b, 64, 1))
+        acc[at + size:at + 2 * size, :] = (
+            tot[HALF + rows.start:HALF + rows.stop, :] + jnp.where(here, pltpu.roll(sum_a, 64, 1), sum_b)
+        )
+        cols = slice(at, FULL if p else 2 * CUT)
+        for i in range(cols.start // 128, cols.stop // 128):
+            flat[:, i * 128:(i + 1) * 128] = acc[i * 128:(i + 1) * 128, :].T
+        for d in (2, 1, 3):
+            for c, pos in enumerate((y, x)):
+                users = pl.ds(pl.multiple_of(64 * c + 16 * turn(pos, d), 16), 16)
+                copy = send(
+                    flat.at[users, cols], fin.at[c, d - 1, :, cols],
+                    fin_send.at[p, c, d - 1], fin_recv.at[p, c, d - 1], axis_peer(1 - c, d),
+                )
+                copy.start()
+                f_copies.append(copy)
     for copy in f_copies:
         copy.wait()
 
@@ -348,7 +366,11 @@
         for c, pos in ((1, x), (0, y)):
             rows = pl.ds(pl.multiple_of(64 * c + 16 * pos, 16), 16)
             mine.insert(0, flat[rows, cols] + fin[c, 0, :, cols] + fin[c, 1, :, cols] + fin[c, 2, :, cols])
-        tot[cols, :] = jnp.concatenate(mine, axis=0).T
+        acc[cols, :] = jnp.concatenate(mine, axis=0).T
+    for rows in pieces:
+        size = rows.stop - rows.start
+        tot[rows, :] = acc[2 * rows.start:2 * rows.start + size, :]
+        tot[HALF + rows.start:HALF + rows.stop, :] = acc[2 * rows.start + size:2 * rows.stop, :]
     solve_tile(tot, lambda j: tot[TRI + j:TRI + j + 1, :], fac, inv, sol)
     turned = jnp.concatenate([sol[...], jnp.zeros((72, 128), jnp.float32)], axis=0).T
     lane = lax.broadcasted_iota(jnp.int32, (16, 128), 1)
@@ -357,69 +379,103 @@
     def w_copy(d):
         return send(pack, w_all.at[col], w_send.at[d], w_recv.at[d], {"col": lax.rem(col + d, count)})
 
-    def send_step(d, carry):
-        w_copy(d).start()
+    def send_step(i, carry):
+        w_copy(1 + lax.rem(i + count // 2 - 1, count - 1)).start()
         return carry
 
-    def wait_step(d, carry):
-        w_copy(d).wait()
-        return carry
-
-    lax.fori_loop(1, count, send_step, 0)
-    w_own = pltpu.make_async_copy(pack, w_all.at[col], w_sem)
+    w_own = pltpu.make_async_copy(pack, w_all.at[col], w_recv.at[0])
     w_own.start()
-    w_ref[...] = turned[:32, :WIDTH]
-    w_own.wait()
-    lax.fori_loop(1, count, wait_step, 0)
-
+    lax.fori_loop(0, count - 1, send_step, 0)
+    w_new[...] = turned[:32, :WIDTH]
+    w_out = pltpu.make_async_copy(w_new, w_hbm, w_sem)
+    w_out.start()
+
+    plane = SIDE * SIDE
     users = 16 * count
-    for i in range(users // 128):
-        wt[:, i * 128:(i + 1) * 128] = w_all[8 * i:8 * i + 8].reshape(128, 128).astype(jnp.float32).T
-    step = users // SIDE
+    step = 16 * plane
     tall = tmp.at[:, 0:step]
     tall[1272:1280, :] = jnp.zeros((8, step), jnp.float32)
 
-    def w_step(i, carry):
-        c = i // SIDE
-        k = i - c * SIDE
-        owner = turn(z, 2 - k + (k // 2) * (2 * k - 1))
-        rows = pl.ds(pl.multiple_of(64 * c, 64), 64)
-        vals = wt[rows, pl.ds(pl.multiple_of(owner * step, step), step)]
-        cols = pl.ds(pl.multiple_of(i * step, step), step)
-        wb[:, cols] = vals.astype(jnp.bfloat16)
-        outer_tile(vals, tall)
-        o_all[:, cols] = tall[...].astype(jnp.bfloat16)
+    def plane_step(t, carry):
+        k = 3 - 2 * t + 3 * (t // 2)
+        owner = turn(z, t + (t // 2) * (5 - 2 * t))
+
+        def arrive_step(i, carry):
+            source = owner * plane + i
+            pltpu.make_async_copy(pack, w_all.at[source], w_recv.at[lax.rem(col - source + count, count)]).wait()
+            return carry
+
+        lax.fori_loop(0, plane, arrive_step, 0)
+        for i in range(step // 128):
+            rows = w_all[pl.ds(owner * plane + 8 * i, 8)].reshape(128, 128)
+            wt[:, i * 128:(i + 1) * 128] = rows.astype(jnp.float32).T
+
+        def colour_step(c, carry):
+            vals = wt[pl.ds(pl.multiple_of(64 * c, 64), 64), :]
+            cols = pl.ds(pl.multiple_of(c * users + k * step, step), step)
+            wb[:, cols] = vals.astype(jnp.bfloat16)
+            outer_tile(vals, tall)
+            o_all[:, cols] = tall[...].astype(jnp.bfloat16)
+            return carry
+
+        lax.fori_loop(0, 2, colour_step, 0)
         return carry
 
-    lax.fori_loop(0, 2 * SIDE, w_step, 0)
+    lax.fori_loop(0, SIDE, plane_step, 0)
     half = items // 2
 
-    def item_partial(side, dst):
+    def item_rows(side, left, m):
         cols = pl.ds(pl.multiple_of(side * half, half), half)
-
-        def both(left, m):
-            total = None
-            for c in range(2):
-                right = mqs[:, :, :, c, m, :, cols].reshape(users, half)
-                term = jnp.dot(left(c), right, preferred_element_type=jnp.float32)
-                total = term if total is None else total + term
-            return total
-
-        dst[TRI:PACK, :] = both(lambda c: wb[:, c * users:(c + 1) * users], 1)
-
-        def rows_step(i, carry):
-            rows = pl.ds(pl.multiple_of(i * 320, 320), 320)
-            dst[rows, :] = both(lambda c: o_all[rows, c * users:(c + 1) * users], 0)
-            return carry
-
-        lax.fori_loop(0, 4, rows_step, 0)
-
-    item_partial(1 - row, part)
-    swap = send(part, swap_got, x_send, x_recv, other)
-    swap.start()
-    item_partial(row, item_ref)
-    swap.wait()
-    item_ref[...] = item_ref[...] + swap_got[...]
+        total = None
+        for c in range(2):
+            right = mqs[:, :, :, c, m, :, cols].reshape(users, half)
+            term = jnp.dot(left(c), right, preferred_element_type=jnp.float32)
+            total = term if total is None else total + term
+        return total
+
+    def rhs_rows(side):
+        return item_rows(side, lambda c: wb[:, c * users:(c + 1) * users], 1)
+
+    def gram_rows(side, rows):
+        return item_rows(side, lambda c: o_all[rows, c * users:(c + 1) * users], 0)
+
+    def swap_copy(i, rows):
+        return send(part.at[rows], swap_got.at[rows], x_send.at[i], x_recv.at[i], other)
+
+    def finish(i, rows, val):
+        swap_copy(i, rows).wait()
+        item_sum[rows, :] = val + swap_got[rows, :]
+        pltpu.make_async_copy(item_sum.at[rows], item_hbm.at[rows], out_sem.at[i]).start()
+
+    tail = pl.ds(TRI, PACK - TRI)
+    part[tail, :] = rhs_rows(1 - row)
+    swap_copy(4, tail).start()
+
+    def away_step(i, carry):
+        rows = pl.ds(pl.multiple_of(i * 320, 320), 320)
+        part[rows, :] = gram_rows(1 - row, rows)
+        swap_copy(i, rows).start()
+        return carry
+
+    def home_step(i, carry):
+        rows = pl.ds(pl.multiple_of(i * 320, 320), 320)
+        finish(i, rows, gram_rows(row, rows))
+        return carry
+
+    lax.fori_loop(0, 4, away_step, 0)
+    finish(4, tail, rhs_rows(row))
+    lax.fori_loop(0, 4, home_step, 0)
+    w_out.wait()
+    for i in range(4):
+        rows = pl.ds(i * 320, 320)
+        pltpu.make_async_copy(item_sum.at[rows], item_hbm.at[rows], out_sem.at[i]).wait()
+    pltpu.make_async_copy(item_sum.at[tail], item_hbm.at[tail], out_sem.at[4]).wait()
+
+    def sent_step(d, carry):
+        w_copy(d).wait_send()
+        return carry
+
+    lax.fori_loop(1, count, sent_step, 0)
 
 
 def half_steps(ratings, mask, vt, count):
@@ -427,7 +483,6 @@
     block = users // SIDE
     dma = pltpu.SemaphoreType.DMA
     any_spec = pl.BlockSpec(memory_space=pl.ANY)
-    vmem_spec = pl.BlockSpec(memory_space=pltpu.VMEM)
     f32, bf16 = jnp.float32, jnp.bfloat16
     return pl.pallas_call(
         als_kernel,
@@ -435,11 +490,12 @@
             jax.ShapeDtypeStruct((32, WIDTH), f32),
             jax.ShapeDtypeStruct((PACK, items // 2), f32),
         ),
-        in_specs=[any_spec, any_spec, vmem_spec],
-        out_specs=(vmem_spec, vmem_spec),
+        in_specs=[any_spec, any_spec, any_spec],
+        out_specs=(any_spec, any_spec),
         scratch_shapes=[
             pltpu.VMEM((4, block, items), f32),
             pltpu.VMEM((4, block, items), jnp.int32),
+            pltpu.VMEM((WIDTH, items), f32),
             pltpu.VMEM((4, SIDE, SIDE, 2, 2, 16, items), bf16),
             pltpu.VMEM((4, 2, 2, SIDE, 16, items), bf16),
             pltpu.VMEM((4, 2, SIDE, 2, 16, 7 * items), bf16),
@@ -450,22 +506,25 @@
             pltpu.VMEM((3, 2, HALF, 128), f32),
             pltpu.VMEM((2, HALF, 128), f32),
             pltpu.VMEM((2, 2, HALF, 128), f32),
+            pltpu.VMEM((PACK, 128), f32),
             pltpu.VMEM((FULL, 128), f32),
             pltpu.VMEM((128, FULL), f32),
             pltpu.VMEM((2, 3, 16, FULL), f32),
             pltpu.VMEM((WIDTH * ROWS, 128), f32),
             pltpu.VMEM((ROWS, 128), f32),
             pltpu.VMEM((ROWS, 128), f32),
+            pltpu.VMEM((32, WIDTH), f32),
             pltpu.VMEM((16, 128), bf16),
             pltpu.VMEM((count, 16, 128), bf16),
-            pltpu.VMEM((128, 16 * count), f32),
+            pltpu.VMEM((128, 16 * SIDE * SIDE), f32),
             pltpu.VMEM((64, 32 * count), bf16),
             pltpu.VMEM((PACK, items // 2), f32),
             pltpu.VMEM((PACK, items // 2), f32),
-            dma((4, 2)), dma((6,)), dma((6,)), dma((4, 2, 2)), dma((4, 2, 2)), dma((4, 2, 2)), dma((4, 2, 2)),
+            pltpu.VMEM((PACK, items // 2), f32),
+            dma, dma((4, 2)), dma((6,)), dma((6,)), dma((4, 2, 2)), dma((4, 2, 2)), dma((4, 2, 2)), dma((4, 2, 2)),
             dma((4, 2, 2)), dma((4, 2, 2)), dma((4, 2)),
-            dma((2, 2)), dma((2, 2)), dma((2, 2, 2)), dma((2, 2, 2)), dma((2, 3)), dma((2, 3)),
-            dma((count,)), dma((count,)), dma, dma, dma,
+            dma((2, 2)), dma((2, 2)), dma((2, 2, 2)), dma((2, 2, 2)), dma((2, 2, 3)), dma((2, 2, 3)),
+            dma((count,)), dma((count,)), dma, dma((5,)), dma((5,)), dma((5,)),
             pltpu.SemaphoreType.REGULAR, pltpu.SemaphoreType.REGULAR,
         ],
         compiler_params=pltpu.CompilerParams(
@@ -482,7 +541,7 @@
 
     def local_als(ratings, mask, v_init):
         w_own, packed = half_steps(ratings, mask, v_init.T, count)
-        v_own = solve_items(packed).T
-        return w_own, v_own
+        v_own, w_own = solve_items(packed, w_own)
+        return w_own, v_own.T
 
     return jax.shard_map(local_als, mesh=mesh, in_specs=in_specs, out_specs=out_specs, check_vma=False)

time: 84.5 us -> 81.2 us (0.961)
  Pallas kernels: 82.3 us -> 80.5 us
  local copies, waits for them, and re-layouts: 1.32 us -> 0 us
    pallas_call x1, Pallas kernels: 75.1 us -> 73.3 us  [half_steps(): pl.pallas_call(als_kernel, out_shape=(jax.ShapeDtypeStruct((32, WIDTH), f...]
    unnamed x1 -> x0, local copies, waits for them, and re-layouts: 1.32 us -> none
where the time goes in v5:
time: 81.2 us; the launch traced here: 81.1 us
  Pallas kernels  80.5 us (99%)
    pallas_call x1, Pallas kernels, half_steps(): pl.pallas_call(als_kernel, out_shape=(jax.ShapeDtypeStruct((32, WIDTH), f...  73.3 us
    pallas_call x1, Pallas kernels, solve_items(): pl.pallas_call(item_solve_kernel, out_shape=(jax.ShapeDtypeStruct((WIDTH,...  7.18 us

profile of v5, /device:TPU:1, one launch (start us, length us, event | category | flops | bytes accessed | tf_op | source)
XLA Modules:
  0.0 81.1 jit_solution(14784921160280861239)
XLA Ops:
  0.6 73.3 %shard_map.50 = (f32[32,50]{1,0:T(8,128)}, f32[1344,256]{1,0:T(8,128)}) custom-call(f32[2048,512]{1,0:T(8,128)} %rate_hbm.1, s32[2048,512]{1,0:T(8,128)} %mask_hbm.1, f32[50,512]{1,0:T(8,128)} %bitcast.2), custom_call_target="tpu_custom_call" | custom-call | tf_op jit(solution)/shard_map/pallas_call | solution.py:487
  73.9 7.2 %shard_map.51 = (f32[50,256]{1,0:T(8,128)}, f32[32,50]{1,0:T(8,128)}) custom-call(f32[1344,256]{1,0:T(8,128)} %get-tuple-element.6.g_ref, f32[32,50]{1,0:T(8,128)} %get-tuple-element.7.w_ref), custom_call_target="tpu_custom_call" | custom-call | tf_op jit(solution)/shard_map/pallas_call | solution.py:93
